TPU v7x, 8 devices: a whole 2x2x1 slice. The times are simulated.
8 devices in a mesh: dp: 1 (over z), m3: 2 (over y), m2: 2 (over x), m1: 2 (over core).
Axes of the slice: x: 2, y: 2, z: 1, core: 2. Of those that a mesh axis runs over, the one named last changes fastest.
Arguments:
- volume: bfloat16 [128, 128, 128, 32], P('dp', 'm1', 'm2', 'm3')
- fac_one: bfloat16 [128, 128], replicated
- fac_two: bfloat16 [128, 128], replicated
- fac_three: bfloat16 [32, 32], replicated
- diag_scale: float32 [32, 128, 128], P('m2', 'm1')
Outputs:
- output: bfloat16 [128, 32, 128, 128], P(('dp', 'm3'), 'm2', 'm1')
All inputs are finite; a program needn't handle non-finite values.
Results may differ from a plain program's by a relative error of at most 0.00844113.
Values are sent between devices in bfloat16 or wider.
A program may use at most 1 GiB of HBM per device.

v0:
```python
import jax
import jax.numpy as jnp
from jax import lax
from jax.sharding import PartitionSpec as P


def solution(mesh):
    def local_step(vol_blk, fac_one, fac_two, fac_three, diag_blk):
        full_three = lax.all_to_all(vol_blk, "m3", 0, 3, tiled=True)
        prod_three = lax.dot_general(full_three, fac_three, (((3,), (1,)), ((), ())), preferred_element_type=jnp.float32).astype(jnp.bfloat16)
        full_two = lax.all_to_all(prod_three, "m2", 3, 2, tiled=True)
        prod_two = lax.dot_general(full_two, fac_two, (((2,), (1,)), ((), ())), preferred_element_type=jnp.float32).astype(jnp.bfloat16)
        full_one = lax.all_to_all(prod_two, "m1", 3, 1, tiled=True)
        prod_one = lax.dot_general(full_one, fac_one, (((1,), (1,)), ((), ())), preferred_element_type=jnp.float32).astype(jnp.bfloat16)
        return (diag_blk[None] * prod_one.astype(jnp.float32)).astype(jnp.bfloat16)

    return jax.shard_map(local_step, mesh=mesh, in_specs=(P("dp", "m1", "m2", "m3"), P(), P(), P(), P("m2", "m1", None)), out_specs=P(("dp", "m3"), "m2", "m1", None), check_vma=False)
```

profile of v0, /device:TPU:0, one launch (start us, length us, event | category | flops | bytes accessed | tf_op | source)
XLA Modules:
  0.0 1075.4 jit_solution(8385928646183381276)
XLA Ops:
  0.0 0.0 copy-start
  0.0 55.1 %copy.15 = bf16[128,64,64,16]{2,3,1,0:T(8,128)(2,1)} copy(bf16[128,64,64,16]{0,3,2,1:T(8,128)(2,1)} %param.5) | data formatting | bytes 33554432 | tf_op args[0]
  55.1 27.9 %reshape.4 = bf16[2,2,2097152]{2,1,0:T(2,128)(2,1)} reshape(bf16[128,64,16,64]{3,2,1,0:T(8,128)(2,1)} %bitcast.44) | data formatting | bytes 33554432
  83.0 202.4 %all_to_all.54 = bf16[2,2,2097152]{2,1,0:T(2,128)(2,1)} all-to-all(bf16[2,2,2097152]{2,1,0:T(2,128)(2,1)} %reshape.4), channel_id=1, replica_groups=mesh['dp'=1,'m3'=2,'m2'=2,'m1'=2] {'m3'}, dimensions={0} | all-to-all | bytes 33554432 | tf_op jit(solution)/shard_map/all_to_all | solution.py:9
  285.4 43.1 %reshape.5 = bf16[128,64,16,64]{3,2,1,0:T(8,128)(2,1)} reshape(bf16[2,2,2097152]{2,1,0:T(2,128)(2,1)} %all_to_all.54) | data formatting | bytes 33554432
  328.6 22.7 %copy.16 = bf16[2,64,64,64,16]{3,4,0,2,1:T(8,128)(2,1)} copy(bf16[2,64,64,64,16]{3,4,2,1,0:T(8,128)(2,1)} %bitcast.45) | data formatting | bytes 33554432 | tf_op jit(solution)/shard_map/all_to_all | solution.py:9
  351.3 0.0 copy-done.3
  351.3 22.9 %convolution_convert_fusion = bf16[64,64,64,32]{2,3,1,0:T(8,128)(2,1)} fusion(bf16[64,64,64,32]{2,3,1,0:T(8,128)(2,1)} %bitcast.42, bf16[32,32]{1,0:T(8,128)(2,1)S(1)} %copy-done.3), kind=kOutput, calls=%fused_computation.3 | convolution fusion | flops 545259520 | bytes 33556480 | tf_op jit(solution)/shard_map/dot_general | solution.py:10
  374.2 23.5 %copy.29 = bf16[64,64,64,32]{2,1,0,3:T(8,128)(2,1)} copy(bf16[64,64,64,32]{2,3,1,0:T(8,128)(2,1)} %convolution_convert_fusion) | data formatting | bytes 33554432 | tf_op jit(solution)/shard_map/convert_element_type | solution.py:10
  397.7 28.1 %reshape.6 = bf16[2,2,2097152]{2,1,0:T(2,128)(2,1)} reshape(bf16[32,64,64,64]{3,2,1,0:T(8,128)(2,1)} %bitcast.46) | data formatting | bytes 33554432
  425.8 199.8 %all_to_all.55 = bf16[2,2,2097152]{2,1,0:T(2,128)(2,1)} all-to-all(bf16[2,2,2097152]{2,1,0:T(2,128)(2,1)} %reshape.6), channel_id=1, replica_groups=mesh['dp'=1,'m3'=2,'m2'=2,'m1'=2] {'m2'}, dimensions={0} | all-to-all | bytes 33554432 | tf_op jit(solution)/shard_map/all_to_all | solution.py:11
  625.6 43.1 %reshape.7 = bf16[32,64,64,64]{3,2,1,0:T(8,128)(2,1)} reshape(bf16[2,2,2097152]{2,1,0:T(2,128)(2,1)} %all_to_all.55) | data formatting | bytes 33554432
  668.7 60.1 %copy.28 = bf16[64,64,64,2,16]{2,3,4,1,0:T(2,128)(2,1)} copy(bf16[64,64,64,2,16]{2,1,0,4,3:T(8,128)(2,1)} %bitcast.47) | data formatting | bytes 33554432 | tf_op jit(solution)/shard_map/all_to_all | solution.py:11
  728.8 52.4 %all_to_all.46 = bf16[64,64,128,16]{2,3,1,0:T(8,128)(2,1)} reshape(bf16[64,64,2,64,16]{3,2,4,1,0:T(2,128)(2,1)} %bitcast.48) | data formatting | bytes 33554432 | tf_op jit(solution)/shard_map/all_to_all | solution.py:11
  781.2 0.0 copy-done
  781.2 11.4 %convolution_convert_fusion.1 = bf16[64,64,16,128]{3,2,1,0:T(8,128)(2,1)} fusion(bf16[64,64,128,16]{2,3,1,0:T(8,128)(2,1)} %all_to_all.46, bf16[128,128]{1,0:T(8,128)(2,1)S(1)} %copy-done), kind=kOutput, calls=%fused_computation.4 | convolution fusion | flops 2155872256 | bytes 33587200 | tf_op jit(solution)/shard_map/dot_general | solution.py:12
  792.6 55.5 %copy.19 = bf16[64,64,16,128]{1,2,0,3:T(8,128)(2,1)} copy(bf16[64,64,16,128]{3,2,1,0:T(8,128)(2,1)} %convolution_convert_fusion.1) | data formatting | bytes 33554432 | tf_op jit(solution)/shard_map/convert_element_type | solution.py:12
  848.1 27.9 %reshape.8 = bf16[2,2,2097152]{2,1,0:T(2,128)(2,1)} reshape(bf16[128,64,16,64]{3,2,1,0:T(8,128)(2,1)} %bitcast.43) | data formatting | bytes 33554432
  876.1 31.5 %all_to_all.56 = bf16[2,2,2097152]{2,1,0:T(2,128)(2,1)} all-to-all(bf16[2,2,2097152]{2,1,0:T(2,128)(2,1)} %reshape.8), channel_id=1, replica_groups=mesh['dp'=1,'m3'=2,'m2'=2,'m1'=2] {'m1'}, dimensions={0} | all-to-all | bytes 33554432 | tf_op jit(solution)/shard_map/all_to_all | solution.py:13
  907.5 43.1 %reshape.9 = bf16[128,64,16,64]{3,2,1,0:T(8,128)(2,1)} reshape(bf16[2,2,2097152]{2,1,0:T(2,128)(2,1)} %all_to_all.56) | data formatting | bytes 33554432
  950.7 60.1 %copy.27 = bf16[64,64,16,2,64]{1,3,4,2,0:T(2,128)(2,1)} copy(bf16[64,64,16,2,64]{1,2,0,4,3:T(8,128)(2,1)} %bitcast.49) | data formatting | bytes 33554432 | tf_op jit(solution)/shard_map/all_to_all | solution.py:13
  1010.8 52.5 %all_to_all.50 = bf16[64,128,16,64]{1,3,2,0:T(8,128)(2,1)} reshape(bf16[64,2,64,16,64]{2,1,4,3,0:T(2,128)(2,1)} %bitcast.50) | data formatting | bytes 33554432 | tf_op jit(solution)/shard_map/all_to_all | solution.py:13
  1063.3 0.0 copy-done.1
  1063.3 11.9 %multiply_convert_fusion = bf16[64,16,64,128]{3,2,1,0:T(8,128)(2,1)} fusion(f32[16,64,128]{2,1,0:T(8,128)S(1)} %copy-done.1, bf16[64,128,16,64]{1,3,2,0:T(8,128)(2,1)} %all_to_all.50, bf16[128,128]{1,0:T(8,128)(2,1)S(1)} %copy-done.2), kind=kOutput, calls=%fused_computation.2 | convolution fusion | flops 2181038080 | bytes 34111488 | tf_op jit(solution)/shard_map/dot_general | solution.py:14
  (4 shorter events, 0.0 us)
Async XLA Ops:
  0.0 781.2 %copy-start = (bf16[128,128]{1,0:T(8,128)(2,1)S(1)}, bf16[128,128]{1,0:T(8,128)(2,1)}, u32[]{:S(2)}) copy-start(bf16[128,128]{1,0:T(8,128)(2,1)} %param.7) | copy-start | bytes 98308
  328.6 22.7 %copy-start.3 = (bf16[32,32]{1,0:T(8,128)(2,1)S(1)}, bf16[32,32]{1,0:T(8,128)(2,1)}, u32[]{:S(2)}) copy-start(bf16[32,32]{1,0:T(8,128)(2,1)} %param.8) | copy-start | bytes 6148
  1010.8 52.5 %copy-start.1 = (f32[16,64,128]{2,1,0:T(8,128)S(1)}, f32[16,64,128]{2,1,0:T(8,128)}, u32[]{:S(2)}) copy-start(f32[16,64,128]{2,1,0:T(8,128)} %param.9) | copy-start | bytes 1572868
  1010.8 52.5 %copy-start.2 = (bf16[128,128]{1,0:T(8,128)(2,1)S(1)}, bf16[128,128]{1,0:T(8,128)(2,1)}, u32[]{:S(2)}) copy-start(bf16[128,128]{1,0:T(8,128)(2,1)} %param.6) | copy-start | bytes 98308
where the time goes:
time: 1090 us; the launch traced here: 1080 us
  local copies, waits for them, and re-layouts  595 us (55%)
  blocking collectives  434 us (40%)
  matrix products  46.3 us (4%)
    unnamed x15, local copies, waits for them, and re-layouts  268 us
    all_to_all x1, blocking collectives, local_step(): full_three = lax.all_to_all(vol_blk, 'm3', 0, 3, tiled=True)  202 us
    all_to_all x1, blocking collectives, local_step(): full_two = lax.all_to_all(prod_three, 'm2', 3, 2, tiled=True)  200 us
    all_to_all x2, local copies, waits for them, and re-layouts, local_step(): full_one = lax.all_to_all(prod_two, 'm1', 3, 1, tiled=True)  113 us
    all_to_all x2, local copies, waits for them, and re-layouts, local_step(): full_two = lax.all_to_all(prod_three, 'm2', 3, 2, tiled=True)  113 us
    convert_element_type x1, local copies, waits for them, and re-layouts, local_step(): lax.dot_general(full_two, fac_two, (((2,), (1,)), ((), ())), preferred_el...  55.5 us
    all_to_all x1, blocking collectives, local_step(): full_one = lax.all_to_all(prod_two, 'm1', 3, 1, tiled=True)  31.5 us
    convert_element_type x1, local copies, waits for them, and re-layouts, local_step(): lax.dot_general(full_three, fac_three, (((3,), (1,)), ((), ())), preferre...  23.5 us

commit v1 on v0

v1 whole, which is shorter than its diff:
```python
import functools

import jax
import jax.numpy as jnp
from jax import lax
from jax.experimental import pallas as pl
from jax.experimental.pallas import tpu as pltpu
from jax.sharding import PartitionSpec as P

MESH = pl.DeviceIdType.MESH
F32, BF16 = jnp.float32, jnp.bfloat16

LANES = 128
SG = 8
AG = 16
RING = 4
BSLAB = 32


def butterfly(tiles, lane_step):
    count = len(tiles)
    lane = lax.broadcasted_iota(jnp.int32, tiles[0].shape, tiles[0].ndim - 1)
    dist = count // 2
    while dist >= 1:
        shift = dist * lane_step
        low = (lane & shift) == 0
        fresh = list(tiles)
        for i in range(count):
            if i & dist:
                continue
            j = i + dist
            axis = tiles[i].ndim - 1
            fresh[i] = jnp.where(low, tiles[i], pltpu.roll(tiles[j], shift, axis))
            fresh[j] = jnp.where(low, pltpu.roll(tiles[i], LANES - shift, axis), tiles[j])
        tiles = fresh
        dist //= 2
    return tiles


def iota(shape, axis):
    return lax.broadcasted_iota(jnp.int32, shape, axis)


def one_hot(cond):
    return jnp.where(cond, 1.0, 0.0).astype(BF16)


def dot(a, b):
    return jnp.dot(a, b, preferred_element_type=F32)


def kernel(x_hbm, a1_ref, a2_ref, a3_ref, d_ref, w_hbm,
           slab, grp, yrecv, u3keep, u3send, xrecv, u2keep, u2send, crecv, wst,
           l3_ref, a2p_ref, a1p_ref,
           slab_sem, w_sem, ysend_sem, yrecv_sem, xsend_sem, xrecv_sem, csend_sem, crecv_sem):
    m3, m2, m1 = lax.axis_index("m3"), lax.axis_index("m2"), lax.axis_index("m1")
    n_a, n_b, n_l, _ = x_hbm.shape
    n_ab = n_a // AG
    n_half = n_b // BSLAB
    n_slab = n_ab * n_half
    n_g = grp.shape[0] // 2
    n_t = n_g * n_ab
    n_k = u3keep.shape[1]
    n_j = u2keep.shape[3]

    def slab_copy(i):
        ab, h = i // n_half, i % n_half
        return pltpu.make_async_copy(
            x_hbm.at[pl.ds(ab * AG, AG), pl.ds(h * BSLAB, BSLAB)], slab.at[i % 2], slab_sem.at[i % 2])

    def y_copy(t):
        g, ab = t // n_ab, t % n_ab
        return pltpu.make_async_remote_copy(
            src_ref=grp.at[(1 - m3) * n_g + g, ab], dst_ref=yrecv.at[t],
            send_sem=ysend_sem.at[t], recv_sem=yrecv_sem.at[t],
            device_id={"m3": 1 - m3}, device_id_type=MESH)

    def x_copy(t):
        return pltpu.make_async_remote_copy(
            src_ref=u3send.at[t % RING], dst_ref=xrecv.at[t],
            send_sem=xsend_sem.at[t % RING], recv_sem=xrecv_sem.at[t],
            device_id={"m2": 1 - m2}, device_id_type=MESH)

    def c_copy(t):
        return pltpu.make_async_remote_copy(
            src_ref=u2send.at[t % RING], dst_ref=crecv.at[t],
            send_sem=csend_sem.at[t % RING], recv_sem=crecv_sem.at[t],
            device_id={"m1": 1 - m1}, device_id_type=MESH)

    def w_copy(g):
        return pltpu.make_async_copy(wst.at[g % 2], w_hbm.at[pl.ds(g * SG, SG)], w_sem.at[g % 2])

    slab_copy(0).start()
    slab_copy(1).start()

    barrier = pltpu.get_barrier_semaphore()
    for partner in ({"m3": 1 - m3}, {"m2": 1 - m2}, {"m1": 1 - m1}):
        pl.semaphore_signal(barrier, inc=1, device_id=partner, device_id_type=MESH)
    pl.semaphore_wait(barrier, 3)

    k_all, l_all = a3_ref.shape
    rows = k_all * 8
    cols = 2 * 8 * n_l
    r, c = iota((rows, k_all), 0), iota((rows, k_all), 1)
    pick_k = one_hot((r // 8 + m2 * n_k) % k_all == c)
    r, c = iota((l_all, cols), 0), iota((l_all, cols), 1)
    pick_l = one_hot((c // (8 * n_l) + m3) % 2 * n_l + c % n_l == r)
    wide = dot(dot(pick_k, a3_ref[...]).astype(BF16), pick_l)
    r, c = iota((rows, cols), 0), iota((rows, cols), 1)
    l3_ref[...] = jnp.where(r % 8 == c // n_l % 8, wide, 0.0).astype(BF16)

    size = a2_ref.shape[0]
    r, c = iota((size, size), 0), iota((size, size), 1)
    pick_j = one_hot((r + m1 * n_j) % size == c)
    pick_b = one_hot((c + m2 * n_b) % size == r)
    a2p_ref[...] = dot(dot(pick_j, a2_ref[...]).astype(BF16), pick_b).astype(BF16)
    v = r % (2 * n_ab)
    pick_a = one_hot((v // n_ab + m1) % 2 * n_a + v % n_ab * AG + r // (2 * n_ab) == c)
    a1p_ref[...] = lax.dot_general(pick_a, a1_ref[...], (((1,), (1,)), ((), ())),
                                   preferred_element_type=F32).astype(BF16)

    def regroup(i, carry):
        ab, h = i // n_half, i % n_half
        slab_copy(i).wait()

        def one_b(b, carry):
            tiles = butterfly([slab[i % 2, a, b] for a in range(AG)], SG)
            for g in range(2 * n_g):
                grp[g, ab, h * BSLAB + b] = tiles[g]
            return carry

        lax.fori_loop(0, BSLAB, one_b, 0)

        @pl.when(i + 2 < n_slab)
        def _():
            slab_copy(i + 2).start()

        @pl.when(h == n_half - 1)
        def _():
            y_copy(ab).start()
        return carry

    lax.fori_loop(0, n_slab, regroup, 0)

    def mode_three(t):
        g, ab = t // n_ab, t % n_ab
        slot = t % RING
        mine = m3 * n_g + g

        def body(bp, carry):
            b0 = bp * 16
            parts = []
            for h in range(2):
                own = grp[mine, ab, pl.ds(b0 + 8 * h, 8)].reshape(8 * n_l, LANES)
                got = yrecv[t, pl.ds(b0 + 8 * h, 8)].reshape(8 * n_l, LANES)
                parts.append(jnp.concatenate([own, got], axis=0))
            out = dot(l3_ref[...], jnp.concatenate(parts, axis=1))
            lo = out[:, :LANES].reshape(2 * n_k, 8, LANES)
            hi = out[:, LANES:].reshape(2 * n_k, 8, LANES)
            full = jnp.concatenate([lo, hi], axis=1).astype(BF16)
            u3keep[slot, :, pl.ds(b0, 16), :] = full[:n_k]
            u3send[slot, :, pl.ds(b0, 16), :] = full[n_k:]
            return carry

        lax.fori_loop(0, n_b // 16, body, 0)

    def mode_two(t):
        g, ab = t // n_ab, t % n_ab
        slot = t % RING

        def body(kp, carry):
            parts = []
            for h in range(2):
                parts.append(jnp.concatenate([u3keep[slot, 2 * kp + h], xrecv[t, 2 * kp + h]], axis=0))
            out = dot(a2p_ref[...], jnp.concatenate(parts, axis=1)).astype(BF16)
            for h in range(2):
                half = out[:, h * LANES:(h + 1) * LANES]
                u2keep[g % 2, ab, 2 * kp + h] = half[:n_j]
                u2send[slot, 2 * kp + h] = half[n_j:]
            return carry

        lax.fori_loop(0, n_k // 2, body, 0)

    def mode_one(g):
        def body(i, carry):
            k, j0 = i // (n_j // 16), i % (n_j // 16) * 16
            tiles = [u2keep[g % 2, ab, k, pl.ds(j0, 16)] for ab in range(n_ab)]
            tiles += [crecv[g * n_ab + ab, k, pl.ds(j0, 16)] for ab in range(n_ab)]
            tiles = butterfly(tiles, 1)
            out = dot(jnp.concatenate(tiles, axis=0), a1p_ref[...]).astype(BF16).astype(F32)
            scale = d_ref[k, pl.ds(j0, 16), :]
            out = (out.reshape(SG, 16, LANES) * scale[None]).astype(BF16)
            wst[g % 2, :, k, pl.ds(j0, 16), :] = out
            return carry

        lax.fori_loop(0, n_k * (n_j // 16), body, 0)

    def step(t, carry):
        @pl.when(t + n_ab < n_t)
        def _():
            y_copy(t + n_ab).start()

        @pl.when(t < n_t)
        def _():
            y_copy(t).wait_recv()

            @pl.when(t >= RING)
            def _():
                x_copy(t - RING).wait_send()
            mode_three(t)
            x_copy(t).start()

        u = t - 1

        @pl.when((u >= 0) & (u < n_t))
        def _():
            x_copy(u).wait_recv()

            @pl.when(u >= RING)
            def _():
                c_copy(u - RING).wait_send()
            mode_two(u)
            c_copy(u).start()

        z = t - 2

        @pl.when((z >= 0) & (z % n_ab == n_ab - 1))
        def _():
            g = z // n_ab

            def wait_core(ab, carry):
                c_copy(g * n_ab + ab).wait_recv()
                return carry
            lax.fori_loop(0, n_ab, wait_core, 0)

            @pl.when(g >= 2)
            def _():
                w_copy(g - 2).wait()
            mode_one(g)
            w_copy(g).start()
        return carry

    lax.fori_loop(0, n_t + 2, step, 0)

    def drain_y(t, carry):
        y_copy(t).wait_send()
        return carry
    lax.fori_loop(0, n_t, drain_y, 0)

    def drain(t, carry):
        x_copy(t).wait_send()
        c_copy(t).wait_send()
        return carry
    lax.fori_loop(n_t - RING, n_t, drain, 0)
    w_copy(n_g - 2).wait()
    w_copy(n_g - 1).wait()


def solution(mesh):
    def local_step(vol_blk, fac_one, fac_two, fac_three, diag_blk):
        n_s, n_a, n_b, n_l = vol_blk.shape
        n_k, n_j, n_i = diag_blk.shape
        x = jnp.transpose(vol_blk, (1, 2, 3, 0))
        n_g = n_s // SG // 2
        n_ab = n_a // AG
        n_t = n_g * n_ab
        vmem = pl.BlockSpec(memory_space=pltpu.VMEM)
        dma = pltpu.SemaphoreType.DMA
        return pl.pallas_call(
            kernel,
            out_shape=jax.ShapeDtypeStruct((n_s // 2, n_k, n_j, n_i), BF16),
            in_specs=[pl.BlockSpec(memory_space=pl.ANY), vmem, vmem, vmem, vmem],
            out_specs=pl.BlockSpec(memory_space=pl.ANY),
            scratch_shapes=[
                pltpu.VMEM((2, AG, BSLAB, n_l, LANES), BF16),
                pltpu.VMEM((2 * n_g, n_ab, n_b, n_l, LANES), BF16),
                pltpu.VMEM((n_t, n_b, n_l, LANES), BF16),
                pltpu.VMEM((RING, n_k, n_b, LANES), BF16),
                pltpu.VMEM((RING, n_k, n_b, LANES), BF16),
                pltpu.VMEM((n_t, n_k, n_b, LANES), BF16),
                pltpu.VMEM((2, n_ab, n_k, n_j, LANES), BF16),
                pltpu.VMEM((RING, n_k, n_j, LANES), BF16),
                pltpu.VMEM((n_t, n_k, n_j, LANES), BF16),
                pltpu.VMEM((2, SG, n_k, n_j, n_i), BF16),
                pltpu.VMEM((fac_three.shape[0] * 8, 2 * 8 * n_l), BF16),
                pltpu.VMEM(fac_two.shape, BF16),
                pltpu.VMEM(fac_one.shape, BF16),
                dma((2,)), dma((2,)),
                dma((n_t,)), dma((n_t,)),
                dma((RING,)), dma((n_t,)),
                dma((RING,)), dma((n_t,)),
            ],
            compiler_params=pltpu.CompilerParams(
                collective_id=0, has_side_effects=True, vmem_limit_bytes=66 * 1024 * 1024 - 4 * 1024 * 1024),
        )(x, fac_one, fac_two, fac_three, diag_blk)

    return jax.shard_map(local_step, mesh=mesh, in_specs=(P("dp", "m1", "m2", "m3"), P(), P(), P(), P("m2", "m1", None)), out_specs=P(("dp", "m3"), "m2", "m1", None), check_vma=False)
```

time: 1090 us -> 450 us (0.41); the launches traced: 1080 us -> 449 us
  local copies, waits for them, and re-layouts: 595 us -> 13.9 us
  Pallas kernels: 0 us -> 435 us
  blocking collectives: 434 us -> 0 us
  matrix products: 46.3 us -> 0 us
    pallas_call x0 -> x1, Pallas kernels: none -> 435 us  [local_step(): pl.pallas_call(kernel, out_shape=jax.ShapeDtypeStruct((n_s // 2, n_k, n_j...]
    all_to_all x3 -> x0, blocking collectives: 434 us -> none  [the longest x1 202 us: local_step(): full_three = lax.all_to_all(vol_blk, 'm3', 0, 3, tiled=True)]
    unnamed x15 -> x1, local copies, waits for them, and re-layouts: 268 us -> 13.9 us
    all_to_all x5 -> x0, local copies, waits for them, and re-layouts: 248 us -> none  [the longest x2 113 us: local_step(): full_one = lax.all_to_all(prod_two, 'm1', 3, 1, tiled=True)]
    convert_element_type x2 -> x0, local copies, waits for them, and re-layouts: 79 us -> none  [the longest x1 55.5 us: local_step(): lax.dot_general(full_two, fac_two, (((2,), (1,)), ((), ())), preferred_el...]
    dot_general x3 -> x0, matrix products: 46.3 us -> none  [the longest x1 22.9 us: local_step(): lax.dot_general(full_three, fac_three, (((3,), (1,)), ((), ())), preferre...]
where the time goes in v1:
time: 450 us; the launch traced here: 449 us
  Pallas kernels  435 us (97%)
  local copies, waits for them, and re-layouts  13.9 us (3%)
    pallas_call x1, Pallas kernels, local_step(): pl.pallas_call(kernel, out_shape=jax.ShapeDtypeStruct((n_s // 2, n_k, n_j...  435 us
    unnamed x1, local copies, waits for them, and re-layouts  13.9 us

profile of v1, /device:TPU:0, one launch (start us, length us, event | category | flops | bytes accessed | tf_op | source)
XLA Modules:
  0.0 448.9 jit_solution(6499213537376219847)
XLA Ops:
  0.0 435.0 %shard_map.55 = bf16[64,16,64,128]{3,2,1,0:T(8,128)(2,1)} custom-call(bf16[64,64,16,128]{3,2,1,0:T(8,128)(2,1)} %bitcast.1, bf16[128,128]{1,0:T(8,128)(2,1)} %a1_ref.1, bf16[128,128]{1,0:T(8,128)(2,1)} %a2_ref.1, bf16[32,32]{1,0:T(8,128)(2,1)} %a3_ref.1, f32[16,64,128]{2,1,0:T(8,128)} %d_ref.1), custom_call_target="tpu_custom_call" | custom-call | tf_op jit(solution)/shard_map/pallas_call | solution.py:269
  435.0 13.9 %copy.7 = bf16[64,16,64,128]{3,2,1,0:T(8,128)(2,1)} copy(bf16[64,16,64,128]{3,2,1,0:T(8,128)(2,1)} %shard_map.55) | data formatting | bytes 33554432

commit v2 on v1

v2 whole, which is shorter than its diff:
```python
import functools

import jax
import jax.numpy as jnp
from jax import lax
from jax.experimental import pallas as pl
from jax.experimental.pallas import tpu as pltpu
from jax.sharding import PartitionSpec as P

MESH = pl.DeviceIdType.MESH
F32, BF16 = jnp.float32, jnp.bfloat16

LANES = 128
SG = 8
AG = 16
RING = 4
PB = 16
U2_RING = 3
PAIRED = 2


def butterfly(tiles, lane_step):
    count = len(tiles)
    lane = lax.broadcasted_iota(jnp.int32, tiles[0].shape, tiles[0].ndim - 1)
    dist = count // 2
    while dist >= 1:
        shift = dist * lane_step
        low = (lane & shift) == 0
        fresh = list(tiles)
        for i in range(count):
            if i & dist:
                continue
            j = i + dist
            axis = tiles[i].ndim - 1
            fresh[i] = jnp.where(low, tiles[i], pltpu.roll(tiles[j], shift, axis))
            fresh[j] = jnp.where(low, pltpu.roll(tiles[i], LANES - shift, axis), tiles[j])
        tiles = fresh
        dist //= 2
    return tiles


def iota(shape, axis):
    return lax.broadcasted_iota(jnp.int32, shape, axis)


def one_hot(cond):
    return jnp.where(cond, 1.0, 0.0).astype(BF16)


def dot(a, b):
    return jnp.dot(a, b, preferred_element_type=F32)


def kernel(x_hbm, a1_ref, a2_ref, a3_ref, d_ref, w_hbm,
           slab, grp, yrecv, u3keep, u3send, xrecv, u2keep, u2send, crecv, wst,
           l3_ref, a2p_ref, a1p_ref,
           slab_sem, w_sem, ysend_sem, yrecv_sem, xsend_sem, xrecv_sem, csend_sem, crecv_sem):
    m3, m2, m1 = lax.axis_index("m3"), lax.axis_index("m2"), lax.axis_index("m1")
    n_a, n_b, n_l, _ = x_hbm.shape
    n_ab = n_a // AG
    n_p = n_b // PB
    n_slab = n_ab * n_p
    n_g = grp.shape[0] // 2
    n_t = n_g * n_ab
    n_k = xrecv.shape[2]
    n_j = u2keep.shape[3]
    k_part = n_k // n_ab
    ahead = n_p - 1

    def place(t):
        early = t < PAIRED * n_ab
        return (jnp.where(early, t % PAIRED, t // n_ab), jnp.where(early, t // PAIRED, t % n_ab))

    def index(g, ab):
        return jnp.where(g < PAIRED, ab * PAIRED + g, g * n_ab + ab)

    def slab_copy(i):
        return pltpu.make_async_copy(
            x_hbm.at[pl.ds(i // n_p * AG, AG), pl.ds(i % n_p * PB, PB)], slab.at[i % RING], slab_sem.at[i % RING])

    def y_copy(t, p):
        g, ab = place(t)
        return pltpu.make_async_remote_copy(
            src_ref=grp.at[(1 - m3) * n_g + g, ab, pl.ds(p * PB, PB)], dst_ref=yrecv.at[t, pl.ds(p * PB, PB)],
            send_sem=ysend_sem.at[t * n_p + p], recv_sem=yrecv_sem.at[t * n_p + p],
            device_id={"m3": 1 - m3}, device_id_type=MESH)

    def x_copy(t, p):
        return pltpu.make_async_remote_copy(
            src_ref=u3send.at[t % RING, p], dst_ref=xrecv.at[t, p],
            send_sem=xsend_sem.at[t % RING * n_p + p], recv_sem=xrecv_sem.at[t * n_p + p],
            device_id={"m2": 1 - m2}, device_id_type=MESH)

    def c_copy(t):
        return pltpu.make_async_remote_copy(
            src_ref=u2send.at[t % RING], dst_ref=crecv.at[t],
            send_sem=csend_sem.at[t % RING], recv_sem=crecv_sem.at[t],
            device_id={"m1": 1 - m1}, device_id_type=MESH)

    def w_copy(n):
        g, part = place(n)
        return pltpu.make_async_copy(
            wst.at[n % RING], w_hbm.at[pl.ds(g * SG, SG), pl.ds(part * k_part, k_part)], w_sem.at[n % RING])

    def each(count, do):
        def body(i, carry):
            do(i)
            return carry
        lax.fori_loop(0, count, body, 0)

    for i in range(RING):
        slab_copy(i).start()

    barrier = pltpu.get_barrier_semaphore()
    for partner in ({"m3": 1 - m3}, {"m2": 1 - m2}, {"m1": 1 - m1}):
        pl.semaphore_signal(barrier, inc=1, device_id=partner, device_id_type=MESH)
    pl.semaphore_wait(barrier, 3)

    def regroup(i):
        ab, p = i // n_p, i % n_p
        slab_copy(i).wait()

        def one_b(b, carry):
            tiles = butterfly([slab[i % RING, a, b] for a in range(AG)], SG)
            for g in range(2 * n_g):
                grp[g, ab, p * PB + b] = tiles[g]
            return carry

        lax.fori_loop(0, PB, one_b, 0, unroll=4)

        @pl.when(i + RING < n_slab)
        def _():
            slab_copy(i + RING).start()

        y_copy(ab * PAIRED, p).start()

        @pl.when(p == n_p - 1)
        def _():
            for e in range(1, PAIRED):
                each(n_p, lambda q: y_copy(ab * PAIRED + e, q).start())

    each(ahead, regroup)

    k_all, l_all = a3_ref.shape
    rows = k_all * 8
    cols = 2 * 8 * n_l
    r, c = iota((rows, k_all), 0), iota((rows, k_all), 1)
    pick_k = one_hot((r // 8 + m2 * n_k) % k_all == c)
    r, c = iota((l_all, cols), 0), iota((l_all, cols), 1)
    pick_l = one_hot((c // (8 * n_l) + m3) % 2 * n_l + c % n_l == r)
    wide = dot(dot(pick_k, a3_ref[...]).astype(BF16), pick_l)
    r, c = iota((rows, cols), 0), iota((rows, cols), 1)
    l3_ref[...] = jnp.where(r % 8 == c // n_l % 8, wide, 0.0).astype(BF16)

    size = a2_ref.shape[0]
    r, c = iota((size, size), 0), iota((size, size), 1)
    pick_j = one_hot((r + m1 * n_j) % size == c)
    pick_b = one_hot((c + m2 * n_b) % size == r)
    a2p_ref[...] = dot(dot(pick_j, a2_ref[...]).astype(BF16), pick_b).astype(BF16)
    v = r % (2 * n_ab)
    pick_a = one_hot((v // n_ab + m1) % 2 * n_a + v % n_ab * AG + r // (2 * n_ab) == c)
    a1p_ref[...] = lax.dot_general(pick_a, a1_ref[...], (((1,), (1,)), ((), ())),
                                   preferred_element_type=F32).astype(BF16)

    def mode_three(t, p):
        g, ab = place(t)
        mine = m3 * n_g + g
        parts = []
        for h in range(2):
            b0 = p * PB + 8 * h
            own = grp[mine, ab, pl.ds(b0, 8)].reshape(8 * n_l, LANES)
            got = yrecv[t, pl.ds(b0, 8)].reshape(8 * n_l, LANES)
            parts.append(jnp.concatenate([own, got], axis=0))
        out = dot(l3_ref[...], jnp.concatenate(parts, axis=1))
        lo = out[:, :LANES].reshape(2 * n_k, 8, LANES)
        hi = out[:, LANES:].reshape(2 * n_k, 8, LANES)
        full = jnp.concatenate([lo, hi], axis=1).astype(BF16)
        u3send[t % RING, p] = full[n_k:]
        u3keep[t % 2, p] = full[:n_k]

    def mode_two(t):
        g, ab = place(t)

        def body(kp, carry):
            parts = []
            for k in (2 * kp, 2 * kp + 1):
                parts.append(jnp.concatenate([u3keep[t % 2, p, k] for p in range(n_p)]
                                             + [xrecv[t, p, k] for p in range(n_p)], axis=0))
            out = dot(a2p_ref[...], jnp.concatenate(parts, axis=1)).astype(BF16)
            for h in range(2):
                half = out[:, h * LANES:(h + 1) * LANES]
                u2send[t % RING, 2 * kp + h] = half[n_j:]
                u2keep[g % U2_RING, ab, 2 * kp + h] = half[:n_j]
            return carry

        lax.fori_loop(0, n_k // 2, body, 0, unroll=n_k // 2)

    def mode_one(n):
        g, part = place(n)

        @pl.when(n >= RING)
        def _():
            w_copy(n - RING).wait()

        def body(i, carry):
            k, j0 = i // (n_j // 16), i % (n_j // 16) * 16
            kk = part * k_part + k
            tiles = [u2keep[g % U2_RING, ab, kk, pl.ds(j0, 16)] for ab in range(n_ab)]
            tiles += [crecv[index(g, ab), kk, pl.ds(j0, 16)] for ab in range(n_ab)]
            tiles = butterfly(tiles, 1)
            out = dot(jnp.concatenate(tiles, axis=0), a1p_ref[...]).astype(BF16).astype(F32)
            scale = d_ref[kk, pl.ds(j0, 16), :]
            out = (out.reshape(SG, 16, LANES) * scale[None]).astype(BF16)
            wst[n % RING, :, k, pl.ds(j0, 16), :] = out
            return carry

        lax.fori_loop(0, k_part * (n_j // 16), body, 0, unroll=8)
        w_copy(n).start()

    def wait_core(g):
        each(n_ab, lambda ab: c_copy(index(g, ab)).wait_recv())

    first = PAIRED * n_ab + 1

    def step(t, carry):
        @pl.when((t + 3 >= PAIRED * n_ab) & (t + 3 < n_t))
        def _():
            each(n_p, lambda p: y_copy(t + 3, p).start())

        def piece(p, carry):
            @pl.when(t < n_t)
            def _():
                y_copy(t, p).wait_recv()

                @pl.when(t >= RING)
                def _():
                    x_copy(t - RING, p).wait_send()
                mode_three(t, p)
                x_copy(t, p).start()

                extra = ahead * (t + 1) + p

                @pl.when((p < ahead) & (extra < n_slab))
                def _():
                    regroup(extra)
            return carry

        lax.fori_loop(0, n_p, piece, 0)

        u = t - 1

        @pl.when(u >= 0)
        def _():
            each(n_p, lambda p: x_copy(u, p).wait_recv())

            @pl.when(u >= RING)
            def _():
                c_copy(u - RING).wait_send()
            mode_two(u)
            c_copy(u).start()

        z = t - first

        @pl.when((z >= 0) & (z < n_ab))
        def _():
            @pl.when(z == 0)
            def _():
                each(PAIRED, wait_core)
            each(PAIRED, lambda e: mode_one(z * PAIRED + e))

        @pl.when(z >= n_ab)
        def _():
            n = z - n_ab + PAIRED * n_ab

            @pl.when(z % n_ab == 0)
            def _():
                wait_core(n // n_ab)
            mode_one(n)
        return carry

    lax.fori_loop(0, n_t + 1, step, 0)

    wait_core(n_g - 1)
    each(n_ab, lambda i: mode_one(n_t - n_ab + i))

    def drain_y(t):
        each(n_p, lambda p: y_copy(t, p).wait_send())
    each(n_t, drain_y)

    def drain(i):
        t = n_t - RING + i
        each(n_p, lambda p: x_copy(t, p).wait_send())
        c_copy(t).wait_send()
        w_copy(t).wait()
    each(RING, drain)


def solution(mesh):
    def local_step(vol_blk, fac_one, fac_two, fac_three, diag_blk):
        n_s, n_a, n_b, n_l = vol_blk.shape
        n_k, n_j, n_i = diag_blk.shape
        x = jnp.transpose(vol_blk, (1, 2, 3, 0))
        n_g = n_s // SG // 2
        n_ab = n_a // AG
        n_t = n_g * n_ab
        n_p = n_b // PB
        vmem = pl.BlockSpec(memory_space=pltpu.VMEM)
        dma = pltpu.SemaphoreType.DMA
        return pl.pallas_call(
            kernel,
            out_shape=jax.ShapeDtypeStruct((n_s // 2, n_k, n_j, n_i), BF16),
            in_specs=[pl.BlockSpec(memory_space=pl.ANY), vmem, vmem, vmem, vmem],
            out_specs=pl.BlockSpec(memory_space=pl.ANY),
            scratch_shapes=[
                pltpu.VMEM((RING, AG, PB, n_l, LANES), BF16),
                pltpu.VMEM((2 * n_g, n_ab, n_b, n_l, LANES), BF16),
                pltpu.VMEM((n_t, n_b, n_l, LANES), BF16),
                pltpu.VMEM((2, n_p, n_k, PB, LANES), BF16),
                pltpu.VMEM((RING, n_p, n_k, PB, LANES), BF16),
                pltpu.VMEM((n_t, n_p, n_k, PB, LANES), BF16),
                pltpu.VMEM((U2_RING, n_ab, n_k, n_j, LANES), BF16),
                pltpu.VMEM((RING, n_k, n_j, LANES), BF16),
                pltpu.VMEM((n_t, n_k, n_j, LANES), BF16),
                pltpu.VMEM((RING, SG, n_k // n_ab, n_j, n_i), BF16),
                pltpu.VMEM((fac_three.shape[0] * 8, 2 * 8 * n_l), BF16),
                pltpu.VMEM(fac_two.shape, BF16),
                pltpu.VMEM(fac_one.shape, BF16),
                dma((RING,)), dma((RING,)),
                dma((n_t * n_p,)), dma((n_t * n_p,)),
                dma((RING * n_p,)), dma((n_t * n_p,)),
                dma((RING,)), dma((n_t,)),
            ],
            compiler_params=pltpu.CompilerParams(
                collective_id=0, has_side_effects=True, vmem_limit_bytes=62 * 1024 * 1024),
        )(x, fac_one, fac_two, fac_three, diag_blk)

    return jax.shard_map(local_step, mesh=mesh, in_specs=(P("dp", "m1", "m2", "m3"), P(), P(), P(), P("m2", "m1", None)), out_specs=P(("dp", "m3"), "m2", "m1", None), check_vma=False)
```

time: 450 us -> 225 us (0.50)
  Pallas kernels: 435 us -> 210 us
    pallas_call x1, Pallas kernels: 435 us -> 210 us  [local_step(): pl.pallas_call(kernel, out_shape=jax.ShapeDtypeStruct((n_s // 2, n_k, n_j...]
where the time goes in v2:
time: 225 us; the launch traced here: 224 us
  Pallas kernels  210 us (93%)
  local copies, waits for them, and re-layouts  13.9 us (6%)
    pallas_call x1, Pallas kernels, local_step(): pl.pallas_call(kernel, out_shape=jax.ShapeDtypeStruct((n_s // 2, n_k, n_j...  210 us
    unnamed x1, local copies, waits for them, and re-layouts  13.9 us

profile of v2, /device:TPU:0, one launch (start us, length us, event | category | flops | bytes accessed | tf_op | source)
XLA Modules:
  0.0 224.4 jit_solution(13819272665935301014)
XLA Ops:
  0.0 210.4 %shard_map.55 = bf16[64,16,64,128]{3,2,1,0:T(8,128)(2,1)} custom-call(bf16[64,64,16,128]{3,2,1,0:T(8,128)(2,1)} %bitcast.1, bf16[128,128]{1,0:T(8,128)(2,1)} %a1_ref.1, bf16[128,128]{1,0:T(8,128)(2,1)} %a2_ref.1, bf16[32,32]{1,0:T(8,128)(2,1)} %a3_ref.1, f32[16,64,128]{2,1,0:T(8,128)} %d_ref.1), custom_call_target="tpu_custom_call" | custom-call | tf_op jit(solution)/shard_map/pallas_call | solution.py:309
  210.5 13.9 %copy.7 = bf16[64,16,64,128]{3,2,1,0:T(8,128)(2,1)} copy(bf16[64,16,64,128]{3,2,1,0:T(8,128)(2,1)} %shard_map.55) | data formatting | bytes 33554432

commit v3 on v2

--- a/solution.py
+++ b/solution.py
@@ -51,10 +51,10 @@
     return jnp.dot(a, b, preferred_element_type=F32)
 
 
-def kernel(x_hbm, a1_ref, a2_ref, a3_ref, d_ref, w_hbm,
-           slab, grp, yrecv, u3keep, u3send, xrecv, u2keep, u2send, crecv, wst,
+def kernel(x_hbm, a1_ref, a2_ref, a3_ref, d_ref, w_ref,
+           slab, grp, yrecv, u3keep, u3send, xrecv, u2keep, u2send, crecv,
            l3_ref, a2p_ref, a1p_ref,
-           slab_sem, w_sem, ysend_sem, yrecv_sem, xsend_sem, xrecv_sem, csend_sem, crecv_sem):
+           slab_sem, free_sem, ysend_sem, yrecv_sem, xsend_sem, xrecv_sem, csend_sem, crecv_sem):
     m3, m2, m1 = lax.axis_index("m3"), lax.axis_index("m2"), lax.axis_index("m1")
     n_a, n_b, n_l, _ = x_hbm.shape
     n_ab = n_a // AG
@@ -91,16 +91,15 @@
             send_sem=xsend_sem.at[t % RING * n_p + p], recv_sem=xrecv_sem.at[t * n_p + p],
             device_id={"m2": 1 - m2}, device_id_type=MESH)
 
+    def room(t):
+        g, ab = place(t)
+        return g % U2_RING * n_ab + ab
+
     def c_copy(t):
         return pltpu.make_async_remote_copy(
-            src_ref=u2send.at[t % RING], dst_ref=crecv.at[t],
+            src_ref=u2send.at[t % RING], dst_ref=crecv.at[room(t)],
             send_sem=csend_sem.at[t % RING], recv_sem=crecv_sem.at[t],
             device_id={"m1": 1 - m1}, device_id_type=MESH)
-
-    def w_copy(n):
-        g, part = place(n)
-        return pltpu.make_async_copy(
-            wst.at[n % RING], w_hbm.at[pl.ds(g * SG, SG), pl.ds(part * k_part, k_part)], w_sem.at[n % RING])
 
     def each(count, do):
         def body(i, carry):
@@ -198,24 +197,23 @@
     def mode_one(n):
         g, part = place(n)
 
-        @pl.when(n >= RING)
-        def _():
-            w_copy(n - RING).wait()
-
         def body(i, carry):
             k, j0 = i // (n_j // 16), i % (n_j // 16) * 16
             kk = part * k_part + k
             tiles = [u2keep[g % U2_RING, ab, kk, pl.ds(j0, 16)] for ab in range(n_ab)]
-            tiles += [crecv[index(g, ab), kk, pl.ds(j0, 16)] for ab in range(n_ab)]
+            tiles += [crecv[g % U2_RING * n_ab + ab, kk, pl.ds(j0, 16)] for ab in range(n_ab)]
             tiles = butterfly(tiles, 1)
             out = dot(jnp.concatenate(tiles, axis=0), a1p_ref[...]).astype(BF16).astype(F32)
             scale = d_ref[kk, pl.ds(j0, 16), :]
             out = (out.reshape(SG, 16, LANES) * scale[None]).astype(BF16)
-            wst[n % RING, :, k, pl.ds(j0, 16), :] = out
+            w_ref[pl.ds(g * SG, SG), kk, pl.ds(j0, 16), :] = out
             return carry
 
         lax.fori_loop(0, k_part * (n_j // 16), body, 0, unroll=8)
-        w_copy(n).start()
+
+        @pl.when((part == n_ab - 1) & (g + U2_RING < n_g))
+        def _():
+            pl.semaphore_signal(free_sem, inc=1, device_id={"m1": 1 - m1}, device_id_type=MESH)
 
     def wait_core(g):
         each(n_ab, lambda ab: c_copy(index(g, ab)).wait_recv())
@@ -257,6 +255,10 @@
             def _():
                 c_copy(u - RING).wait_send()
             mode_two(u)
+
+            @pl.when((u % n_ab == 0) & (u >= U2_RING * n_ab))
+            def _():
+                pl.semaphore_wait(free_sem, 1)
             c_copy(u).start()
 
         z = t - first
@@ -291,7 +293,6 @@
         t = n_t - RING + i
         each(n_p, lambda p: x_copy(t, p).wait_send())
         c_copy(t).wait_send()
-        w_copy(t).wait()
     each(RING, drain)
 
 
@@ -308,9 +309,9 @@
         dma = pltpu.SemaphoreType.DMA
         return pl.pallas_call(
             kernel,
-            out_shape=jax.ShapeDtypeStruct((n_s // 2, n_k, n_j, n_i), BF16),
+            out_shape=pltpu.VMEM((n_s // 2, n_k, n_j, n_i), BF16),
             in_specs=[pl.BlockSpec(memory_space=pl.ANY), vmem, vmem, vmem, vmem],
-            out_specs=pl.BlockSpec(memory_space=pl.ANY),
+            out_specs=vmem,
             scratch_shapes=[
                 pltpu.VMEM((RING, AG, PB, n_l, LANES), BF16),
                 pltpu.VMEM((2 * n_g, n_ab, n_b, n_l, LANES), BF16),
@@ -320,18 +321,17 @@
                 pltpu.VMEM((n_t, n_p, n_k, PB, LANES), BF16),
                 pltpu.VMEM((U2_RING, n_ab, n_k, n_j, LANES), BF16),
                 pltpu.VMEM((RING, n_k, n_j, LANES), BF16),
-                pltpu.VMEM((n_t, n_k, n_j, LANES), BF16),
-                pltpu.VMEM((RING, SG, n_k // n_ab, n_j, n_i), BF16),
+                pltpu.VMEM((U2_RING * n_ab, n_k, n_j, LANES), BF16),
                 pltpu.VMEM((fac_three.shape[0] * 8, 2 * 8 * n_l), BF16),
                 pltpu.VMEM(fac_two.shape, BF16),
                 pltpu.VMEM(fac_one.shape, BF16),
-                dma((RING,)), dma((RING,)),
+                dma((RING,)), pltpu.SemaphoreType.REGULAR,
                 dma((n_t * n_p,)), dma((n_t * n_p,)),
                 dma((RING * n_p,)), dma((n_t * n_p,)),
                 dma((RING,)), dma((n_t,)),
             ],
             compiler_params=pltpu.CompilerParams(
-                collective_id=0, has_side_effects=True, vmem_limit_bytes=62 * 1024 * 1024),
+                collective_id=0, has_side_effects=True, vmem_limit_bytes=47 * 1024 * 1024),
         )(x, fac_one, fac_two, fac_three, diag_blk)
 
     return jax.shard_map(local_step, mesh=mesh, in_specs=(P("dp", "m1", "m2", "m3"), P(), P(), P(), P("m2", "m1", None)), out_specs=P(("dp", "m3"), "m2", "m1", None), check_vma=False)

time: 225 us -> 217 us (0.964)
  local copies, waits for them, and re-layouts: 13.9 us -> 6.16 us
    unnamed x1, local copies, waits for them, and re-layouts: 13.9 us -> 6.16 us
where the time goes in v3:
time: 217 us; the launch traced here: 216 us
  Pallas kernels  210 us (97%)
  local copies, waits for them, and re-layouts  6.16 us (3%)
    pallas_call x1, Pallas kernels, local_step(): pl.pallas_call(kernel, out_shape=pltpu.VMEM((n_s // 2, n_k, n_j, n_i), BF...  210 us
    unnamed x1, local copies, waits for them, and re-layouts  6.16 us

profile of v3, /device:TPU:0, one launch (start us, length us, event | category | flops | bytes accessed | tf_op | source)
XLA Modules:
  0.0 216.4 jit_solution(8131943342049728233)
XLA Ops:
  0.0 210.2 %shard_map.55 = bf16[64,16,64,128]{3,2,1,0:T(8,128)(2,1)S(1)} custom-call(bf16[64,64,16,128]{3,2,1,0:T(8,128)(2,1)} %bitcast.1, bf16[128,128]{1,0:T(8,128)(2,1)} %a1_ref.1, bf16[128,128]{1,0:T(8,128)(2,1)} %a2_ref.1, bf16[32,32]{1,0:T(8,128)(2,1)} %a3_ref.1, f32[16,64,128]{2,1,0:T(8,128)} %d_ref.1), custom_call_target="tpu_custom_call" | custom-call | tf_op jit(solution)/shard_map/pallas_call | solution.py:310
  210.2 6.2 %copy.7 = bf16[64,16,64,128]{3,2,1,0:T(8,128)(2,1)} copy(bf16[64,16,64,128]{3,2,1,0:T(8,128)(2,1)S(1)} %shard_map.55) | data formatting | bytes 33554432

commit v4 on v3

v4 whole, which is shorter than its diff:
```python
import jax
import jax.numpy as jnp
from jax import lax
from jax.experimental import pallas as pl
from jax.experimental.pallas import tpu as pltpu
from jax.sharding import PartitionSpec as P

MESH = pl.DeviceIdType.MESH
F32, BF16 = jnp.float32, jnp.bfloat16

LANES = 128
SG = 8
AG = 16
PB = 16
SLAB_RING = 4
Y_RING = 6
X_RING = 4
C_RING = 4
G_RING = 3
Y_AHEAD = 2
PRE = 3
PER = 2


def skew(tiles, step):
    count = len(tiles)
    axis = tiles[0].ndim - 1
    block = lax.broadcasted_iota(jnp.int32, tiles[0].shape, axis) // step
    tiles = [t if i == 0 else pltpu.roll(t, i * step, axis) for i, t in enumerate(tiles)]
    dist = 1
    while dist < count:
        on = (block & dist) != 0
        tiles = [jnp.where(on, tiles[(h + dist) % count], tiles[h]) for h in range(count)]
        dist *= 2
    return [tiles[(count - g) % count] for g in range(count)]


def exchange(tiles, step):
    axis = tiles[0].ndim - 1
    return [t if g == 0 else pltpu.roll(t, LANES - g * step, axis) for g, t in enumerate(skew(tiles, step))]


def iota(shape, axis):
    return lax.broadcasted_iota(jnp.int32, shape, axis)


def one_hot(cond):
    return jnp.where(cond, 1.0, 0.0).astype(BF16)


def dot(a, b):
    return jnp.dot(a, b, preferred_element_type=F32)


def each(count, do):
    def body(i, carry):
        do(i)
        return carry
    lax.fori_loop(0, count, body, 0)


def kernel(x_hbm, a1_ref, a2_ref, a3_ref, d_ref, w_ref,
           slab, grp, yrecv, u3keep, u3send, xrecv, u2keep, u2send, crecv,
           l3_ref, a2p_ref, a1p_ref,
           slab_sem, free_sem, ysend_sem, yrecv_sem, xsend_sem, xrecv_sem, csend_sem, crecv_sem):
    m3, m2, m1 = lax.axis_index("m3"), lax.axis_index("m2"), lax.axis_index("m1")
    n_a, n_b, n_l, _ = x_hbm.shape
    n_ab = n_a // AG
    n_p = n_b // PB
    n_slab = n_ab * n_p
    n_g = grp.shape[0] // 2
    n_t = n_g * n_ab
    n_k = xrecv.shape[2]
    n_j = u2keep.shape[3]
    k_part = n_k // n_ab

    def slab_copy(i):
        return pltpu.make_async_copy(
            x_hbm.at[pl.ds(i // n_p * AG, AG), pl.ds(i % n_p * PB, PB)],
            slab.at[i % SLAB_RING], slab_sem.at[i % SLAB_RING])

    def y_copy(t, p):
        return pltpu.make_async_remote_copy(
            src_ref=grp.at[(1 - m3) * n_g + t // n_ab, t % n_ab, pl.ds(p * PB, PB)],
            dst_ref=yrecv.at[t, pl.ds(p * PB, PB)],
            send_sem=ysend_sem.at[t % Y_RING * n_p + p], recv_sem=yrecv_sem.at[t % Y_RING * n_p + p],
            device_id={"m3": 1 - m3}, device_id_type=MESH)

    def x_copy(t, p):
        return pltpu.make_async_remote_copy(
            src_ref=u3send.at[t % X_RING, p], dst_ref=xrecv.at[t, p],
            send_sem=xsend_sem.at[t % X_RING * n_p + p], recv_sem=xrecv_sem.at[t % X_RING * n_p + p],
            device_id={"m2": 1 - m2}, device_id_type=MESH)

    def c_copy(t):
        room = t % (G_RING * n_ab)
        return pltpu.make_async_remote_copy(
            src_ref=u2send.at[t % C_RING], dst_ref=crecv.at[room],
            send_sem=csend_sem.at[t % C_RING], recv_sem=crecv_sem.at[room],
            device_id={"m1": 1 - m1}, device_id_type=MESH)

    for i in range(SLAB_RING):
        slab_copy(i).start()

    barrier = pltpu.get_barrier_semaphore()
    for partner in ({"m3": 1 - m3}, {"m2": 1 - m2}, {"m1": 1 - m1}):
        pl.semaphore_signal(barrier, inc=1, device_id=partner, device_id_type=MESH)

    def regroup(i):
        ab, p = i // n_p, i % n_p
        slab_copy(i).wait()

        def one_b(b, carry):
            tiles = skew([slab[i % SLAB_RING, a, b] for a in range(AG)], SG)
            for g in range(2 * n_g):
                grp[g, ab, p * PB + b] = tiles[g]
            return carry

        lax.fori_loop(0, PB, one_b, 0, unroll=4)

        @pl.when(i + SLAB_RING < n_slab)
        def _():
            slab_copy(i + SLAB_RING).start()

    def regroup_send(i):
        regroup(i)
        y_copy(i // n_p, i % n_p).start()

    regroup(0)
    pl.semaphore_wait(barrier, 3)
    y_copy(0, 0).start()
    each(PRE - 1, lambda i: regroup_send(i + 1))

    k_all, l_all = a3_ref.shape
    rows = k_all * 8
    cols = 2 * 8 * n_l
    r, c = iota((rows, k_all), 0), iota((rows, k_all), 1)
    pick_k = one_hot((r // 8 + m2 * n_k) % k_all == c)
    r, c = iota((l_all, cols), 0), iota((l_all, cols), 1)
    pick_l = one_hot((c // (8 * n_l) + m3) % 2 * n_l + c % n_l == r)
    wide = dot(dot(pick_k, a3_ref[...]).astype(BF16), pick_l)
    r, c = iota((rows, cols), 0), iota((rows, cols), 1)
    l3_ref[...] = jnp.where(r % 8 == c // n_l % 8, wide, 0.0).astype(BF16)

    def order_two():
        size = a2_ref.shape[0]
        r, c = iota((size, size), 0), iota((size, size), 1)
        pick_j = one_hot((r + m1 * n_j) % size == c)
        pick_b = one_hot((c + m2 * n_b) % size == r)
        a2p_ref[...] = dot(dot(pick_j, a2_ref[...]).astype(BF16), pick_b).astype(BF16)

    def order_one(g):
        size = a1_ref.shape[0]
        r, c = iota((size, size), 0), iota((size, size), 1)
        v = r % (2 * n_ab)
        in_block = (r // (2 * n_ab) + 2 * n_g - (m3 * n_g + g)) % AG
        pick_a = one_hot((v // n_ab + m1) % 2 * n_a + v % n_ab * AG + in_block == c)
        a1p_ref[g] = lax.dot_general(pick_a, a1_ref[...], (((1,), (1,)), ((), ())),
                                     preferred_element_type=F32).astype(BF16)

    def mode_three(t, p):
        mine = m3 * n_g + t // n_ab
        parts = []
        for h in range(2):
            b0 = p * PB + 8 * h
            own = grp[mine, t % n_ab, pl.ds(b0, 8)].reshape(8 * n_l, LANES)
            got = yrecv[t, pl.ds(b0, 8)].reshape(8 * n_l, LANES)
            parts.append(jnp.concatenate([own, got], axis=0))
        out = dot(l3_ref[...], jnp.concatenate(parts, axis=1))
        lo = out[:, :LANES].reshape(2 * n_k, 8, LANES)
        hi = out[:, LANES:].reshape(2 * n_k, 8, LANES)
        full = jnp.concatenate([lo, hi], axis=1).astype(BF16)
        u3send[t % X_RING, p] = full[n_k:]
        u3keep[t % 2, p] = full[:n_k]

    def mode_two(t):
        g, ab = t // n_ab, t % n_ab

        def body(kp, carry):
            parts = []
            for k in (2 * kp, 2 * kp + 1):
                parts.append(jnp.concatenate([u3keep[t % 2, p, k] for p in range(n_p)]
                                             + [xrecv[t, p, k] for p in range(n_p)], axis=0))
            out = dot(a2p_ref[...], jnp.concatenate(parts, axis=1)).astype(BF16)
            for h in range(2):
                half = out[:, h * LANES:(h + 1) * LANES]
                u2send[t % C_RING, 2 * kp + h] = half[n_j:]
                u2keep[g % G_RING, ab, 2 * kp + h] = half[:n_j]
            return carry

        lax.fori_loop(0, n_k // 2, body, 0, unroll=n_k // 2)

    def mode_one(n):
        g, part = n // n_ab, n % n_ab
        slot = g % G_RING

        def body(i, carry):
            k, j0 = part * k_part + i // (n_j // 16), i % (n_j // 16) * 16
            tiles = [u2keep[slot, ab, k, pl.ds(j0, 16)] for ab in range(n_ab)]
            tiles += [crecv[slot * n_ab + ab, k, pl.ds(j0, 16)] for ab in range(n_ab)]
            tiles = exchange(tiles, 1)
            out = dot(jnp.concatenate(tiles, axis=0), a1p_ref[g]).astype(BF16).astype(F32)
            scale = d_ref[k, pl.ds(j0, 16), :]
            out = (out.reshape(SG, 16, LANES) * scale[None]).astype(BF16)
            w_ref[pl.ds(g * SG, SG), k, pl.ds(j0, 16), :] = out
            return carry

        count = k_part * (n_j // 16)
        lax.fori_loop(0, count, body, 0, unroll=count)

        @pl.when((part == n_ab - 1) & (g + G_RING < n_g))
        def _():
            pl.semaphore_signal(free_sem, inc=1, device_id={"m1": 1 - m1}, device_id_type=MESH)

    def wait_core(g):
        each(n_ab, lambda ab: c_copy(g * n_ab + ab).wait_recv())

    def step(t, carry):
        @pl.when((t + Y_AHEAD >= n_ab) & (t + Y_AHEAD < n_t))
        def _():
            @pl.when(t + Y_AHEAD >= Y_RING)
            def _():
                each(n_p, lambda p: y_copy(t + Y_AHEAD - Y_RING, p).wait_send())
            each(n_p, lambda p: y_copy(t + Y_AHEAD, p).start())

        def piece(p):
            y_copy(t, p).wait_recv()

            @pl.when(t >= X_RING)
            def _():
                x_copy(t - X_RING, p).wait_send()
            mode_three(t, p)
            x_copy(t, p).start()

            extra = PRE + PER * (t * n_p + p)

            @pl.when(extra < n_slab)
            def _():
                each(jnp.minimum(PER, n_slab - extra), lambda e: regroup_send(extra + e))

        @pl.when(t < n_t)
        def _():
            each(n_p, piece)

        @pl.when(t == 0)
        def _():
            order_two()

        u = t - 1

        @pl.when(u >= 0)
        def _():
            each(n_p, lambda p: x_copy(u, p).wait_recv())

            @pl.when(u >= C_RING)
            def _():
                c_copy(u - C_RING).wait_send()
            mode_two(u)

            @pl.when((u % n_ab == 0) & (u >= G_RING * n_ab))
            def _():
                pl.semaphore_wait(free_sem, 1)
            c_copy(u).start()

        @pl.when(t < n_g)
        def _():
            order_one(t)

        n = t - n_ab - 1

        @pl.when(n >= 0)
        def _():
            @pl.when(n % n_ab == 0)
            def _():
                wait_core(n // n_ab)
            mode_one(n)
        return carry

    lax.fori_loop(0, n_t + 1, step, 0)

    wait_core(n_g - 1)
    each(n_ab, lambda i: mode_one(n_t - n_ab + i))

    def drain_y(i):
        each(n_p, lambda p: y_copy(n_t - Y_RING + i, p).wait_send())
    each(Y_RING, drain_y)
    each(X_RING, lambda i: each(n_p, lambda p: x_copy(n_t - X_RING + i, p).wait_send()))
    each(C_RING, lambda i: c_copy(n_t - C_RING + i).wait_send())


def solution(mesh):
    def local_step(vol_blk, fac_one, fac_two, fac_three, diag_blk):
        n_s, n_a, n_b, n_l = vol_blk.shape
        n_k, n_j, n_i = diag_blk.shape
        x = jnp.transpose(vol_blk, (1, 2, 3, 0))
        n_g = n_s // SG // 2
        n_ab = n_a // AG
        n_t = n_g * n_ab
        n_p = n_b // PB
        vmem = pl.BlockSpec(memory_space=pltpu.VMEM)
        dma = pltpu.SemaphoreType.DMA
        return pl.pallas_call(
            kernel,
            out_shape=pltpu.VMEM((n_s // 2, n_k, n_j, n_i), BF16),
            in_specs=[pl.BlockSpec(memory_space=pl.ANY), vmem, vmem, vmem, vmem],
            out_specs=vmem,
            scratch_shapes=[
                pltpu.VMEM((SLAB_RING, AG, PB, n_l, LANES), BF16),
                pltpu.VMEM((2 * n_g, n_ab, n_b, n_l, LANES), BF16),
                pltpu.VMEM((n_t, n_b, n_l, LANES), BF16),
                pltpu.VMEM((2, n_p, n_k, PB, LANES), BF16),
                pltpu.VMEM((X_RING, n_p, n_k, PB, LANES), BF16),
                pltpu.VMEM((n_t, n_p, n_k, PB, LANES), BF16),
                pltpu.VMEM((G_RING, n_ab, n_k, n_j, LANES), BF16),
                pltpu.VMEM((C_RING, n_k, n_j, LANES), BF16),
                pltpu.VMEM((G_RING * n_ab, n_k, n_j, LANES), BF16),
                pltpu.VMEM((fac_three.shape[0] * 8, 2 * 8 * n_l), BF16),
                pltpu.VMEM(fac_two.shape, BF16),
                pltpu.VMEM((n_g,) + fac_one.shape, BF16),
                dma((SLAB_RING,)), pltpu.SemaphoreType.REGULAR,
                dma((Y_RING * n_p,)), dma((Y_RING * n_p,)),
                dma((X_RING * n_p,)), dma((X_RING * n_p,)),
                dma((C_RING,)), dma((G_RING * n_ab,)),
            ],
            compiler_params=pltpu.CompilerParams(
                collective_id=0, has_side_effects=True, vmem_limit_bytes=47 * 1024 * 1024),
        )(x, fac_one, fac_two, fac_three, diag_blk)

    return jax.shard_map(local_step, mesh=mesh, in_specs=(P("dp", "m1", "m2", "m3"), P(), P(), P(), P("m2", "m1", None)), out_specs=P(("dp", "m3"), "m2", "m1", None), check_vma=False)
```

time: 217 us -> 203 us (0.935)
  Pallas kernels: 210 us -> 196 us
    pallas_call x1, Pallas kernels: 210 us -> 196 us  [local_step(): pl.pallas_call(kernel, out_shape=pltpu.VMEM((n_s // 2, n_k, n_j, n_i), BF...]
where the time goes in v4:
time: 203 us
  Pallas kernels  196 us (97%)
  local copies, waits for them, and re-layouts  6.16 us (3%)
    pallas_call x1, Pallas kernels, local_step(): pl.pallas_call(kernel, out_shape=pltpu.VMEM((n_s // 2, n_k, n_j, n_i), BF...  196 us
    unnamed x1, local copies, waits for them, and re-layouts  6.16 us

profile of v4, /device:TPU:0, one launch (start us, length us, event | category | flops | bytes accessed | tf_op | source)
XLA Modules:
  0.0 202.5 jit_solution(18054277366428210750)
XLA Ops:
  0.0 196.4 %shard_map.55 = bf16[64,16,64,128]{3,2,1,0:T(8,128)(2,1)S(1)} custom-call(bf16[64,64,16,128]{3,2,1,0:T(8,128)(2,1)} %bitcast.1, bf16[128,128]{1,0:T(8,128)(2,1)} %a1_ref.1, bf16[128,128]{1,0:T(8,128)(2,1)} %a2_ref.1, bf16[32,32]{1,0:T(8,128)(2,1)} %a3_ref.1, f32[16,64,128]{2,1,0:T(8,128)} %d_ref.1), custom_call_target="tpu_custom_call" | custom-call | tf_op jit(solution)/shard_map/pallas_call | solution.py:302
  196.4 6.2 %copy.7 = bf16[64,16,64,128]{3,2,1,0:T(8,128)(2,1)} copy(bf16[64,16,64,128]{3,2,1,0:T(8,128)(2,1)S(1)} %shard_map.55) | data formatting | bytes 33554432

commit v5 on v4

--- a/solution.py
+++ b/solution.py
@@ -13,11 +13,11 @@
 AG = 16
 PB = 16
 SLAB_RING = 4
-Y_RING = 6
+Y_RING = 18
 X_RING = 4
 C_RING = 4
-G_RING = 3
-Y_AHEAD = 2
+CR_RING = 12
+Y_AHEAD = 8
 PRE = 3
 PER = 2
 
@@ -59,10 +59,24 @@
     lax.fori_loop(0, count, body, 0)
 
 
-def kernel(x_hbm, a1_ref, a2_ref, a3_ref, d_ref, w_ref,
-           slab, grp, yrecv, u3keep, u3send, xrecv, u2keep, u2send, crecv,
-           l3_ref, a2p_ref, a1p_ref,
-           slab_sem, free_sem, ysend_sem, yrecv_sem, xsend_sem, xrecv_sem, csend_sem, crecv_sem):
+def mode_one_part(src, dst, a1p, d_ref, k_src, k_dst, count):
+    n_jt = d_ref.shape[1] // 16
+
+    def body(i, carry):
+        k, rows = i // n_jt, pl.ds(i % n_jt * 16, 16)
+        tiles = exchange([src[v, k_src + k, rows] for v in range(SG)], 1)
+        out = dot(jnp.concatenate(tiles, axis=0), a1p).astype(BF16).astype(F32)
+        out = out.reshape(SG, 16, LANES) * d_ref[k_src + k, rows, :][None]
+        dst[:, k_dst + k, rows, :] = out.astype(BF16)
+        return carry
+
+    lax.fori_loop(0, count * n_jt, body, 0, unroll=count * n_jt)
+
+
+def kernel(x_hbm, a1_ref, a2_ref, a3_ref, d_ref, w_ref, a1p_ref,
+           slab, grp, yrecv, u3keep, u3send, xrecv, u2send,
+           l3_ref, a2p_ref,
+           slab_sem, ysend_sem, yrecv_sem, xsend_sem, xrecv_sem, csend_sem, crecv_sem):
     m3, m2, m1 = lax.axis_index("m3"), lax.axis_index("m2"), lax.axis_index("m1")
     n_a, n_b, n_l, _ = x_hbm.shape
     n_ab = n_a // AG
@@ -71,7 +85,7 @@
     n_g = grp.shape[0] // 2
     n_t = n_g * n_ab
     n_k = xrecv.shape[2]
-    n_j = u2keep.shape[3]
+    n_j = u2send.shape[2]
     k_part = n_k // n_ab
 
     def slab_copy(i):
@@ -79,11 +93,12 @@
             x_hbm.at[pl.ds(i // n_p * AG, AG), pl.ds(i % n_p * PB, PB)],
             slab.at[i % SLAB_RING], slab_sem.at[i % SLAB_RING])
 
-    def y_copy(t, p):
+    def y_copy(q):
+        t, p = q // n_p, q % n_p
         return pltpu.make_async_remote_copy(
             src_ref=grp.at[(1 - m3) * n_g + t // n_ab, t % n_ab, pl.ds(p * PB, PB)],
             dst_ref=yrecv.at[t, pl.ds(p * PB, PB)],
-            send_sem=ysend_sem.at[t % Y_RING * n_p + p], recv_sem=yrecv_sem.at[t % Y_RING * n_p + p],
+            send_sem=ysend_sem.at[q % Y_RING], recv_sem=yrecv_sem.at[q % Y_RING],
             device_id={"m3": 1 - m3}, device_id_type=MESH)
 
     def x_copy(t, p):
@@ -93,14 +108,12 @@
             device_id={"m2": 1 - m2}, device_id_type=MESH)
 
     def c_copy(t):
-        room = t % (G_RING * n_ab)
         return pltpu.make_async_remote_copy(
-            src_ref=u2send.at[t % C_RING], dst_ref=crecv.at[room],
-            send_sem=csend_sem.at[t % C_RING], recv_sem=crecv_sem.at[room],
+            src_ref=u2send.at[t % C_RING], dst_ref=w_ref.at[t // n_ab * SG + n_ab + t % n_ab],
+            send_sem=csend_sem.at[t % C_RING], recv_sem=crecv_sem.at[t % CR_RING],
             device_id={"m1": 1 - m1}, device_id_type=MESH)
 
-    for i in range(SLAB_RING):
-        slab_copy(i).start()
+    slab_copy(0).start()
 
     barrier = pltpu.get_barrier_semaphore()
     for partner in ({"m3": 1 - m3}, {"m2": 1 - m2}, {"m1": 1 - m1}):
@@ -108,8 +121,6 @@
 
     def regroup(i):
         ab, p = i // n_p, i % n_p
-        slab_copy(i).wait()
-
         def one_b(b, carry):
             tiles = skew([slab[i % SLAB_RING, a, b] for a in range(AG)], SG)
             for g in range(2 * n_g):
@@ -123,12 +134,16 @@
             slab_copy(i + SLAB_RING).start()
 
     def regroup_send(i):
+        slab_copy(i).wait()
         regroup(i)
-        y_copy(i // n_p, i % n_p).start()
-
+        y_copy(i).start()
+
+    slab_copy(0).wait()
+    for i in range(1, SLAB_RING):
+        slab_copy(i).start()
     regroup(0)
     pl.semaphore_wait(barrier, 3)
-    y_copy(0, 0).start()
+    y_copy(0).start()
     each(PRE - 1, lambda i: regroup_send(i + 1))
 
     k_all, l_all = a3_ref.shape
@@ -185,46 +200,30 @@
             for h in range(2):
                 half = out[:, h * LANES:(h + 1) * LANES]
                 u2send[t % C_RING, 2 * kp + h] = half[n_j:]
-                u2keep[g % G_RING, ab, 2 * kp + h] = half[:n_j]
+                w_ref[g * SG + ab, 2 * kp + h] = half[:n_j]
             return carry
 
         lax.fori_loop(0, n_k // 2, body, 0, unroll=n_k // 2)
 
     def mode_one(n):
         g, part = n // n_ab, n % n_ab
-        slot = g % G_RING
-
-        def body(i, carry):
-            k, j0 = part * k_part + i // (n_j // 16), i % (n_j // 16) * 16
-            tiles = [u2keep[slot, ab, k, pl.ds(j0, 16)] for ab in range(n_ab)]
-            tiles += [crecv[slot * n_ab + ab, k, pl.ds(j0, 16)] for ab in range(n_ab)]
-            tiles = exchange(tiles, 1)
-            out = dot(jnp.concatenate(tiles, axis=0), a1p_ref[g]).astype(BF16).astype(F32)
-            scale = d_ref[k, pl.ds(j0, 16), :]
-            out = (out.reshape(SG, 16, LANES) * scale[None]).astype(BF16)
-            w_ref[pl.ds(g * SG, SG), k, pl.ds(j0, 16), :] = out
-            return carry
-
-        count = k_part * (n_j // 16)
-        lax.fori_loop(0, count, body, 0, unroll=count)
-
-        @pl.when((part == n_ab - 1) & (g + G_RING < n_g))
-        def _():
-            pl.semaphore_signal(free_sem, inc=1, device_id={"m1": 1 - m1}, device_id_type=MESH)
+        here = w_ref.at[pl.ds(g * SG, SG)]
+        mode_one_part(here, here, a1p_ref[g], d_ref, part * k_part, part * k_part, k_part)
 
     def wait_core(g):
         each(n_ab, lambda ab: c_copy(g * n_ab + ab).wait_recv())
 
     def step(t, carry):
-        @pl.when((t + Y_AHEAD >= n_ab) & (t + Y_AHEAD < n_t))
-        def _():
-            @pl.when(t + Y_AHEAD >= Y_RING)
-            def _():
-                each(n_p, lambda p: y_copy(t + Y_AHEAD - Y_RING, p).wait_send())
-            each(n_p, lambda p: y_copy(t + Y_AHEAD, p).start())
-
         def piece(p):
-            y_copy(t, p).wait_recv()
+            q = t * n_p + p
+            y_copy(q).wait_recv()
+
+            @pl.when((q + Y_AHEAD >= n_slab) & (q + Y_AHEAD < n_t * n_p))
+            def _():
+                @pl.when(q + Y_AHEAD >= Y_RING)
+                def _():
+                    y_copy(q + Y_AHEAD - Y_RING).wait_send()
+                y_copy(q + Y_AHEAD).start()
 
             @pl.when(t >= X_RING)
             def _():
@@ -232,7 +231,7 @@
             mode_three(t, p)
             x_copy(t, p).start()
 
-            extra = PRE + PER * (t * n_p + p)
+            extra = PRE + PER * q
 
             @pl.when(extra < n_slab)
             def _():
@@ -256,10 +255,6 @@
             def _():
                 c_copy(u - C_RING).wait_send()
             mode_two(u)
-
-            @pl.when((u % n_ab == 0) & (u >= G_RING * n_ab))
-            def _():
-                pl.semaphore_wait(free_sem, 1)
             c_copy(u).start()
 
         @pl.when(t < n_g)
@@ -278,14 +273,36 @@
 
     lax.fori_loop(0, n_t + 1, step, 0)
 
-    wait_core(n_g - 1)
-    each(n_ab, lambda i: mode_one(n_t - n_ab + i))
-
-    def drain_y(i):
-        each(n_p, lambda p: y_copy(n_t - Y_RING + i, p).wait_send())
-    each(Y_RING, drain_y)
+    last = n_t * n_p - Y_RING
+    each(Y_RING, lambda i: y_copy(last + i).wait_send())
     each(X_RING, lambda i: each(n_p, lambda p: x_copy(n_t - X_RING + i, p).wait_send()))
     each(C_RING, lambda i: c_copy(n_t - C_RING + i).wait_send())
+    wait_core(n_g - 1)
+
+
+def finish(w_vmem, a1p_ref, d_ref, w_hbm, wst, w_sem, last_sem):
+    n_g = w_vmem.shape[0] // SG
+    n_k = w_vmem.shape[1]
+    parts = last_sem.shape[0]
+    k_part = n_k // parts
+
+    def group_copy(g):
+        here = pl.ds(g * SG, SG)
+        return pltpu.make_async_copy(w_vmem.at[here], w_hbm.at[here], w_sem.at[g])
+
+    def part_copy(i):
+        return pltpu.make_async_copy(
+            wst.at[i], w_hbm.at[pl.ds((n_g - 1) * SG, SG), pl.ds(i * k_part, k_part)], last_sem.at[i])
+
+    each(n_g - 1, lambda g: group_copy(g).start())
+    a1p = a1p_ref[n_g - 1]
+
+    def part(i):
+        mode_one_part(w_vmem.at[pl.ds((n_g - 1) * SG, SG)], wst.at[i], a1p, d_ref, i * k_part, 0, k_part)
+        part_copy(i).start()
+    each(parts, part)
+    each(n_g - 1, lambda g: group_copy(g).wait())
+    each(parts, lambda i: part_copy(i).wait())
 
 
 def solution(mesh):
@@ -299,11 +316,11 @@
         n_p = n_b // PB
         vmem = pl.BlockSpec(memory_space=pltpu.VMEM)
         dma = pltpu.SemaphoreType.DMA
-        return pl.pallas_call(
+        w_vmem, a1p = pl.pallas_call(
             kernel,
-            out_shape=pltpu.VMEM((n_s // 2, n_k, n_j, n_i), BF16),
+            out_shape=(pltpu.VMEM((n_s // 2, n_k, n_j, n_i), BF16), pltpu.VMEM((n_g,) + fac_one.shape, BF16)),
             in_specs=[pl.BlockSpec(memory_space=pl.ANY), vmem, vmem, vmem, vmem],
-            out_specs=vmem,
+            out_specs=(vmem, vmem),
             scratch_shapes=[
                 pltpu.VMEM((SLAB_RING, AG, PB, n_l, LANES), BF16),
                 pltpu.VMEM((2 * n_g, n_ab, n_b, n_l, LANES), BF16),
@@ -311,19 +328,24 @@
                 pltpu.VMEM((2, n_p, n_k, PB, LANES), BF16),
                 pltpu.VMEM((X_RING, n_p, n_k, PB, LANES), BF16),
                 pltpu.VMEM((n_t, n_p, n_k, PB, LANES), BF16),
-                pltpu.VMEM((G_RING, n_ab, n_k, n_j, LANES), BF16),
                 pltpu.VMEM((C_RING, n_k, n_j, LANES), BF16),
-                pltpu.VMEM((G_RING * n_ab, n_k, n_j, LANES), BF16),
                 pltpu.VMEM((fac_three.shape[0] * 8, 2 * 8 * n_l), BF16),
                 pltpu.VMEM(fac_two.shape, BF16),
-                pltpu.VMEM((n_g,) + fac_one.shape, BF16),
-                dma((SLAB_RING,)), pltpu.SemaphoreType.REGULAR,
-                dma((Y_RING * n_p,)), dma((Y_RING * n_p,)),
+                dma((SLAB_RING,)),
+                dma((Y_RING,)), dma((Y_RING,)),
                 dma((X_RING * n_p,)), dma((X_RING * n_p,)),
-                dma((C_RING,)), dma((G_RING * n_ab,)),
+                dma((C_RING,)), dma((CR_RING,)),
             ],
             compiler_params=pltpu.CompilerParams(
-                collective_id=0, has_side_effects=True, vmem_limit_bytes=47 * 1024 * 1024),
+                collective_id=0, has_side_effects=True, vmem_limit_bytes=43 * 1024 * 1024),
         )(x, fac_one, fac_two, fac_three, diag_blk)
+        return pl.pallas_call(
+            finish,
+            out_shape=jax.ShapeDtypeStruct(w_vmem.shape, BF16),
+            in_specs=[vmem, vmem, vmem],
+            out_specs=pl.BlockSpec(memory_space=pl.ANY),
+            scratch_shapes=[pltpu.VMEM((n_ab, SG, n_k // n_ab, n_j, n_i), BF16), dma((n_g,)), dma((n_ab,))],
+            compiler_params=pltpu.CompilerParams(vmem_limit_bytes=8 * 1024 * 1024),
+        )(w_vmem, a1p, diag_blk)
 
     return jax.shard_map(local_step, mesh=mesh, in_specs=(P("dp", "m1", "m2", "m3"), P(), P(), P(), P("m2", "m1", None)), out_specs=P(("dp", "m3"), "m2", "m1", None), check_vma=False)

time: 203 us -> 200 us (0.985)
  local copies, waits for them, and re-layouts: 6.16 us -> 0.01 us
  Pallas kernels: 196 us -> 200 us
    unnamed x1 -> x2, local copies, waits for them, and re-layouts: 6.16 us -> 0.01 us
    pallas_call x1 -> x2, Pallas kernels: 196 us -> 200 us  [the longest x1 194 us: local_step(): pl.pallas_call(kernel, out_shape=(pltpu.VMEM((n_s // 2, n_k, n_j, n_i), B...]
where the time goes in v5:
time: 200 us
  Pallas kernels  200 us (100%)
    pallas_call x1, Pallas kernels, local_step(): pl.pallas_call(kernel, out_shape=(pltpu.VMEM((n_s // 2, n_k, n_j, n_i), B...  194 us
    pallas_call x1, Pallas kernels, local_step(): pl.pallas_call(finish, out_shape=jax.ShapeDtypeStruct(w_vmem.shape, BF16)...  5.91 us

profile of v5, /device:TPU:0, one launch (start us, length us, event | category | flops | bytes accessed | tf_op | source)
XLA Modules:
  0.0 200.3 jit_solution(14729253508024558041)
XLA Ops:
  0.0 0.0 copy-start
  0.0 194.4 %shard_map.55 = (bf16[64,16,64,128]{3,2,1,0:T(8,128)(2,1)S(1)}, bf16[8,128,128]{2,1,0:T(8,128)(2,1)S(1)}) custom-call(bf16[64,64,16,128]{3,2,1,0:T(8,128)(2,1)} %bitcast.1, bf16[128,128]{1,0:T(8,128)(2,1)} %a1_ref.1, bf16[128,128]{1,0:T(8,128)(2,1)} %a2_ref.1, bf16[32,32]{1,0:T(8,128)(2,1)} %a3_ref.1, f32[16,64,128]{2,1,0:T(8,128)} %d_ref.3), custom_call_target="tpu_custom_call" | custom-call | tf_op jit(solution)/shard_map/pallas_call | solution.py:319
  194.4 0.0 copy-done
  194.4 5.9 %shard_map.56 = bf16[64,16,64,128]{3,2,1,0:T(8,128)(2,1)} custom-call(bf16[64,16,64,128]{3,2,1,0:T(8,128)(2,1)S(1)} %get-tuple-element.7.w_vmem, bf16[8,128,128]{2,1,0:T(8,128)(2,1)S(1)} %get-tuple-element.8.a1p_ref, f32[16,64,128]{2,1,0:T(8,128)S(1)} %copy-done), custom_call_target="tpu_custom_call" | custom-call | tf_op jit(solution)/shard_map/pallas_call | solution.py:342
Async XLA Ops:
  0.0 194.4 %copy-start = (f32[16,64,128]{2,1,0:T(8,128)S(1)}, f32[16,64,128]{2,1,0:T(8,128)}, u32[]{:S(2)}) copy-start(f32[16,64,128]{2,1,0:T(8,128)} %d_ref.3) | copy-start | bytes 1572868

commit v6 on v5

--- a/solution.py
+++ b/solution.py
@@ -11,15 +11,14 @@
 LANES = 128
 SG = 8
 AG = 16
-PB = 16
-SLAB_RING = 4
-Y_RING = 18
+PB = 8
+SLAB_RING = 8
+FIRST = 2
+AHEAD = 8
+Y_RING = 16
 X_RING = 4
 C_RING = 4
-CR_RING = 12
-Y_AHEAD = 8
-PRE = 3
-PER = 2
+CG_RING = 3
 
 
 def skew(tiles, step):
@@ -93,27 +92,41 @@
             x_hbm.at[pl.ds(i // n_p * AG, AG), pl.ds(i % n_p * PB, PB)],
             slab.at[i % SLAB_RING], slab_sem.at[i % SLAB_RING])
 
+    def remote(axis, src, dst, send_sem, recv_sem):
+        return pltpu.make_async_remote_copy(
+            src_ref=src, dst_ref=dst, send_sem=send_sem, recv_sem=recv_sem,
+            device_id={axis: 1 - lax.axis_index(axis)}, device_id_type=MESH)
+
     def y_copy(q):
         t, p = q // n_p, q % n_p
-        return pltpu.make_async_remote_copy(
-            src_ref=grp.at[(1 - m3) * n_g + t // n_ab, t % n_ab, pl.ds(p * PB, PB)],
-            dst_ref=yrecv.at[t, pl.ds(p * PB, PB)],
-            send_sem=ysend_sem.at[q % Y_RING], recv_sem=yrecv_sem.at[q % Y_RING],
-            device_id={"m3": 1 - m3}, device_id_type=MESH)
+        return remote("m3", grp.at[(1 - m3) * n_g + t // n_ab, t % n_ab, pl.ds(p * PB, PB)],
+                      yrecv.at[t // n_ab, t % n_ab, pl.ds(p * PB, PB)], ysend_sem, yrecv_sem.at[q % Y_RING])
+
+    def y_all():
+        return remote("m3", grp.at[pl.ds((1 - m3) * n_g, n_g)], yrecv, ysend_sem, yrecv_sem.at[0])
 
     def x_copy(t, p):
-        return pltpu.make_async_remote_copy(
-            src_ref=u3send.at[t % X_RING, p], dst_ref=xrecv.at[t, p],
-            send_sem=xsend_sem.at[t % X_RING * n_p + p], recv_sem=xrecv_sem.at[t % X_RING * n_p + p],
-            device_id={"m2": 1 - m2}, device_id_type=MESH)
-
-    def c_copy(t):
-        return pltpu.make_async_remote_copy(
-            src_ref=u2send.at[t % C_RING], dst_ref=w_ref.at[t // n_ab * SG + n_ab + t % n_ab],
-            send_sem=csend_sem.at[t % C_RING], recv_sem=crecv_sem.at[t % CR_RING],
-            device_id={"m1": 1 - m1}, device_id_type=MESH)
-
-    slab_copy(0).start()
+        return remote("m2", u3send.at[t % X_RING, p], xrecv.at[t, p],
+                      xsend_sem.at[t % X_RING], xrecv_sem.at[t % X_RING])
+
+    def x_all(t):
+        return remote("m2", u3send.at[t % X_RING], xrecv.at[t],
+                      xsend_sem.at[t % X_RING], xrecv_sem.at[t % X_RING])
+
+    def c_copy(t, ks):
+        g = t // n_ab
+        return remote("m1", u2send.at[t % C_RING, ks], w_ref.at[g * SG + n_ab + t % n_ab, ks],
+                      csend_sem.at[t % C_RING], crecv_sem.at[g % CG_RING])
+
+    def c_sent(t):
+        return c_copy(t, pl.ds(0, n_k))
+
+    def c_group(g):
+        here = w_ref.at[pl.ds(g * SG + n_ab, n_ab)]
+        return remote("m1", here, here, csend_sem.at[0], crecv_sem.at[g % CG_RING])
+
+    for i in range(FIRST):
+        slab_copy(i).start()
 
     barrier = pltpu.get_barrier_semaphore()
     for partner in ({"m3": 1 - m3}, {"m2": 1 - m2}, {"m1": 1 - m1}):
@@ -133,18 +146,21 @@
         def _():
             slab_copy(i + SLAB_RING).start()
 
-    def regroup_send(i):
-        slab_copy(i).wait()
-        regroup(i)
-        y_copy(i).start()
-
     slab_copy(0).wait()
-    for i in range(1, SLAB_RING):
+    for i in range(FIRST, SLAB_RING):
         slab_copy(i).start()
     regroup(0)
     pl.semaphore_wait(barrier, 3)
     y_copy(0).start()
-    each(PRE - 1, lambda i: regroup_send(i + 1))
+
+    def next_piece(i):
+        @pl.when(i < n_slab)
+        def _():
+            slab_copy(i).wait()
+            regroup(i)
+        y_copy(i).start()
+
+    each(AHEAD - 1, lambda i: next_piece(i + 1))
 
     k_all, l_all = a3_ref.shape
     rows = k_all * 8
@@ -174,68 +190,48 @@
                                      preferred_element_type=F32).astype(BF16)
 
     def mode_three(t, p):
-        mine = m3 * n_g + t // n_ab
-        parts = []
-        for h in range(2):
-            b0 = p * PB + 8 * h
-            own = grp[mine, t % n_ab, pl.ds(b0, 8)].reshape(8 * n_l, LANES)
-            got = yrecv[t, pl.ds(b0, 8)].reshape(8 * n_l, LANES)
-            parts.append(jnp.concatenate([own, got], axis=0))
-        out = dot(l3_ref[...], jnp.concatenate(parts, axis=1))
-        lo = out[:, :LANES].reshape(2 * n_k, 8, LANES)
-        hi = out[:, LANES:].reshape(2 * n_k, 8, LANES)
-        full = jnp.concatenate([lo, hi], axis=1).astype(BF16)
-        u3send[t % X_RING, p] = full[n_k:]
-        u3keep[t % 2, p] = full[:n_k]
+        g, ab, rows = t // n_ab, t % n_ab, pl.ds(p * PB, PB)
+        own = grp[m3 * n_g + g, ab, rows].reshape(PB * n_l, LANES)
+        got = yrecv[g, ab, rows].reshape(PB * n_l, LANES)
+        out = dot(l3_ref[...], jnp.concatenate([own, got], axis=0))
+        out = out.reshape(2 * n_k, PB, LANES).astype(BF16)
+        u3send[t % X_RING, p] = out[n_k:]
+        u3keep[t % 2, p] = out[:n_k]
 
     def mode_two(t):
         g, ab = t // n_ab, t % n_ab
-
-        def body(kp, carry):
-            parts = []
-            for k in (2 * kp, 2 * kp + 1):
-                parts.append(jnp.concatenate([u3keep[t % 2, p, k] for p in range(n_p)]
-                                             + [xrecv[t, p, k] for p in range(n_p)], axis=0))
-            out = dot(a2p_ref[...], jnp.concatenate(parts, axis=1)).astype(BF16)
-            for h in range(2):
-                half = out[:, h * LANES:(h + 1) * LANES]
-                u2send[t % C_RING, 2 * kp + h] = half[n_j:]
-                w_ref[g * SG + ab, 2 * kp + h] = half[:n_j]
-            return carry
-
-        lax.fori_loop(0, n_k // 2, body, 0, unroll=n_k // 2)
+        for part in range(n_ab):
+            for kp in range(part * k_part, (part + 1) * k_part, 2):
+                cols = []
+                for k in (kp, kp + 1):
+                    cols.append(jnp.concatenate([u3keep[t % 2, :, k].reshape(n_b, LANES),
+                                                 xrecv[t, :, k].reshape(n_b, LANES)], axis=0))
+                out = dot(a2p_ref[...], jnp.concatenate(cols, axis=1)).astype(BF16)
+                for h in range(2):
+                    half = out[:, h * LANES:(h + 1) * LANES]
+                    u2send[t % C_RING, kp + h] = half[n_j:]
+                    w_ref[g * SG + ab, kp + h] = half[:n_j]
+            c_copy(t, pl.ds(part * k_part, k_part)).start()
 
     def mode_one(n):
         g, part = n // n_ab, n % n_ab
         here = w_ref.at[pl.ds(g * SG, SG)]
         mode_one_part(here, here, a1p_ref[g], d_ref, part * k_part, part * k_part, k_part)
 
-    def wait_core(g):
-        each(n_ab, lambda ab: c_copy(g * n_ab + ab).wait_recv())
-
     def step(t, carry):
+        @pl.when((t >= X_RING) & (t < n_t))
+        def _():
+            x_all(t - X_RING).wait_send()
+
         def piece(p):
             q = t * n_p + p
             y_copy(q).wait_recv()
-
-            @pl.when((q + Y_AHEAD >= n_slab) & (q + Y_AHEAD < n_t * n_p))
-            def _():
-                @pl.when(q + Y_AHEAD >= Y_RING)
-                def _():
-                    y_copy(q + Y_AHEAD - Y_RING).wait_send()
-                y_copy(q + Y_AHEAD).start()
-
-            @pl.when(t >= X_RING)
-            def _():
-                x_copy(t - X_RING, p).wait_send()
             mode_three(t, p)
             x_copy(t, p).start()
 
-            extra = PRE + PER * q
-
-            @pl.when(extra < n_slab)
+            @pl.when(q + AHEAD < n_t * n_p)
             def _():
-                each(jnp.minimum(PER, n_slab - extra), lambda e: regroup_send(extra + e))
+                next_piece(q + AHEAD)
 
         @pl.when(t < n_t)
         def _():
@@ -249,13 +245,12 @@
 
         @pl.when(u >= 0)
         def _():
-            each(n_p, lambda p: x_copy(u, p).wait_recv())
+            x_all(u).wait_recv()
 
             @pl.when(u >= C_RING)
             def _():
-                c_copy(u - C_RING).wait_send()
+                c_sent(u - C_RING).wait_send()
             mode_two(u)
-            c_copy(u).start()
 
         @pl.when(t < n_g)
         def _():
@@ -267,17 +262,16 @@
         def _():
             @pl.when(n % n_ab == 0)
             def _():
-                wait_core(n // n_ab)
+                c_group(n // n_ab).wait_recv()
             mode_one(n)
         return carry
 
     lax.fori_loop(0, n_t + 1, step, 0)
 
-    last = n_t * n_p - Y_RING
-    each(Y_RING, lambda i: y_copy(last + i).wait_send())
-    each(X_RING, lambda i: each(n_p, lambda p: x_copy(n_t - X_RING + i, p).wait_send()))
-    each(C_RING, lambda i: c_copy(n_t - C_RING + i).wait_send())
-    wait_core(n_g - 1)
+    y_all().wait_send()
+    each(X_RING, lambda i: x_all(n_t - X_RING + i).wait_send())
+    each(C_RING, lambda i: c_sent(n_t - C_RING + i).wait_send())
+    c_group(n_g - 1).wait_recv()
 
 
 def finish(w_vmem, a1p_ref, d_ref, w_hbm, wst, w_sem, last_sem):
@@ -324,7 +318,7 @@
             scratch_shapes=[
                 pltpu.VMEM((SLAB_RING, AG, PB, n_l, LANES), BF16),
                 pltpu.VMEM((2 * n_g, n_ab, n_b, n_l, LANES), BF16),
-                pltpu.VMEM((n_t, n_b, n_l, LANES), BF16),
+                pltpu.VMEM((n_g, n_ab, n_b, n_l, LANES), BF16),
                 pltpu.VMEM((2, n_p, n_k, PB, LANES), BF16),
                 pltpu.VMEM((X_RING, n_p, n_k, PB, LANES), BF16),
                 pltpu.VMEM((n_t, n_p, n_k, PB, LANES), BF16),
@@ -332,9 +326,9 @@
                 pltpu.VMEM((fac_three.shape[0] * 8, 2 * 8 * n_l), BF16),
                 pltpu.VMEM(fac_two.shape, BF16),
                 dma((SLAB_RING,)),
-                dma((Y_RING,)), dma((Y_RING,)),
-                dma((X_RING * n_p,)), dma((X_RING * n_p,)),
-                dma((C_RING,)), dma((CR_RING,)),
+                dma, dma((Y_RING,)),
+                dma((X_RING,)), dma((X_RING,)),
+                dma((C_RING,)), dma((CG_RING,)),
             ],
             compiler_params=pltpu.CompilerParams(
                 collective_id=0, has_side_effects=True, vmem_limit_bytes=43 * 1024 * 1024),

time: 200 us -> 199 us (level)
  Pallas kernels: 200 us -> 198 us
where the time goes in v6:
time: 199 us; the launch traced here: 198 us
  Pallas kernels  198 us (99%)
    pallas_call x1, Pallas kernels, local_step(): pl.pallas_call(kernel, out_shape=(pltpu.VMEM((n_s // 2, n_k, n_j, n_i), B...  193 us
    pallas_call x1, Pallas kernels, local_step(): pl.pallas_call(finish, out_shape=jax.ShapeDtypeStruct(w_vmem.shape, BF16)...  5.91 us

profile of v6, /device:TPU:0, one launch (start us, length us, event | category | flops | bytes accessed | tf_op | source)
XLA Modules:
  0.0 198.5 jit_solution(14972597474339058605)
XLA Ops:
  0.0 0.0 copy-start
  0.0 192.5 %shard_map.55 = (bf16[64,16,64,128]{3,2,1,0:T(8,128)(2,1)S(1)}, bf16[8,128,128]{2,1,0:T(8,128)(2,1)S(1)}) custom-call(bf16[64,64,16,128]{3,2,1,0:T(8,128)(2,1)} %bitcast.1, bf16[128,128]{1,0:T(8,128)(2,1)} %a1_ref.1, bf16[128,128]{1,0:T(8,128)(2,1)} %a2_ref.1, bf16[32,32]{1,0:T(8,128)(2,1)} %a3_ref.1, f32[16,64,128]{2,1,0:T(8,128)} %d_ref.3), custom_call_target="tpu_custom_call" | custom-call | tf_op jit(solution)/shard_map/pallas_call | solution.py:313
  192.6 0.0 copy-done
  192.6 5.9 %shard_map.56 = bf16[64,16,64,128]{3,2,1,0:T(8,128)(2,1)} custom-call(bf16[64,16,64,128]{3,2,1,0:T(8,128)(2,1)S(1)} %get-tuple-element.7.w_vmem, bf16[8,128,128]{2,1,0:T(8,128)(2,1)S(1)} %get-tuple-element.8.a1p_ref, f32[16,64,128]{2,1,0:T(8,128)S(1)} %copy-done), custom_call_target="tpu_custom_call" | custom-call | tf_op jit(solution)/shard_map/pallas_call | solution.py:336
Async XLA Ops:
  0.0 192.6 %copy-start = (f32[16,64,128]{2,1,0:T(8,128)S(1)}, f32[16,64,128]{2,1,0:T(8,128)}, u32[]{:S(2)}) copy-start(f32[16,64,128]{2,1,0:T(8,128)} %d_ref.3) | copy-start | bytes 1572868

commit v7 on v6

--- a/solution.py
+++ b/solution.py
@@ -12,12 +12,12 @@
 SG = 8
 AG = 16
 PB = 8
-SLAB_RING = 8
-FIRST = 2
-AHEAD = 8
-Y_RING = 16
+SLAB_RING = 4
+FIRST = 4
+AHEAD = 7
+Y_RING = 14
 X_RING = 4
-C_RING = 4
+C_RING = 2
 CG_RING = 3
 
 
@@ -113,13 +113,10 @@
         return remote("m2", u3send.at[t % X_RING], xrecv.at[t],
                       xsend_sem.at[t % X_RING], xrecv_sem.at[t % X_RING])
 
-    def c_copy(t, ks):
+    def c_copy(t):
         g = t // n_ab
-        return remote("m1", u2send.at[t % C_RING, ks], w_ref.at[g * SG + n_ab + t % n_ab, ks],
+        return remote("m1", u2send.at[t % C_RING], w_ref.at[g * SG + n_ab + t % n_ab],
                       csend_sem.at[t % C_RING], crecv_sem.at[g % CG_RING])
-
-    def c_sent(t):
-        return c_copy(t, pl.ds(0, n_k))
 
     def c_group(g):
         here = w_ref.at[pl.ds(g * SG + n_ab, n_ab)]
@@ -140,7 +137,7 @@
                 grp[g, ab, p * PB + b] = tiles[g]
             return carry
 
-        lax.fori_loop(0, PB, one_b, 0, unroll=4)
+        lax.fori_loop(0, PB, one_b, 0, unroll=8)
 
         @pl.when(i + SLAB_RING < n_slab)
         def _():
@@ -200,18 +197,17 @@
 
     def mode_two(t):
         g, ab = t // n_ab, t % n_ab
-        for part in range(n_ab):
-            for kp in range(part * k_part, (part + 1) * k_part, 2):
-                cols = []
-                for k in (kp, kp + 1):
-                    cols.append(jnp.concatenate([u3keep[t % 2, :, k].reshape(n_b, LANES),
-                                                 xrecv[t, :, k].reshape(n_b, LANES)], axis=0))
-                out = dot(a2p_ref[...], jnp.concatenate(cols, axis=1)).astype(BF16)
-                for h in range(2):
-                    half = out[:, h * LANES:(h + 1) * LANES]
-                    u2send[t % C_RING, kp + h] = half[n_j:]
-                    w_ref[g * SG + ab, kp + h] = half[:n_j]
-            c_copy(t, pl.ds(part * k_part, k_part)).start()
+        for kp in range(0, n_k, 2):
+            cols = []
+            for k in (kp, kp + 1):
+                cols.append(jnp.concatenate([u3keep[t % 2, :, k].reshape(n_b, LANES),
+                                             xrecv[t, :, k].reshape(n_b, LANES)], axis=0))
+            out = dot(a2p_ref[...], jnp.concatenate(cols, axis=1)).astype(BF16)
+            for h in range(2):
+                half = out[:, h * LANES:(h + 1) * LANES]
+                u2send[t % C_RING, kp + h] = half[n_j:]
+                w_ref[g * SG + ab, kp + h] = half[:n_j]
+        c_copy(t).start()
 
     def mode_one(n):
         g, part = n // n_ab, n % n_ab
@@ -249,7 +245,7 @@
 
             @pl.when(u >= C_RING)
             def _():
-                c_sent(u - C_RING).wait_send()
+                c_copy(u - C_RING).wait_send()
             mode_two(u)
 
         @pl.when(t < n_g)
@@ -270,23 +266,23 @@
 
     y_all().wait_send()
     each(X_RING, lambda i: x_all(n_t - X_RING + i).wait_send())
-    each(C_RING, lambda i: c_sent(n_t - C_RING + i).wait_send())
+    each(C_RING, lambda i: c_copy(n_t - C_RING + i).wait_send())
     c_group(n_g - 1).wait_recv()
 
 
 def finish(w_vmem, a1p_ref, d_ref, w_hbm, wst, w_sem, last_sem):
     n_g = w_vmem.shape[0] // SG
     n_k = w_vmem.shape[1]
-    parts = last_sem.shape[0]
+    parts = wst.shape[0]
     k_part = n_k // parts
 
     def group_copy(g):
         here = pl.ds(g * SG, SG)
-        return pltpu.make_async_copy(w_vmem.at[here], w_hbm.at[here], w_sem.at[g])
+        return pltpu.make_async_copy(w_vmem.at[here], w_hbm.at[here], w_sem)
 
     def part_copy(i):
         return pltpu.make_async_copy(
-            wst.at[i], w_hbm.at[pl.ds((n_g - 1) * SG, SG), pl.ds(i * k_part, k_part)], last_sem.at[i])
+            wst.at[i], w_hbm.at[pl.ds((n_g - 1) * SG, SG), pl.ds(i * k_part, k_part)], last_sem)
 
     each(n_g - 1, lambda g: group_copy(g).start())
     a1p = a1p_ref[n_g - 1]
@@ -295,8 +291,10 @@
         mode_one_part(w_vmem.at[pl.ds((n_g - 1) * SG, SG)], wst.at[i], a1p, d_ref, i * k_part, 0, k_part)
         part_copy(i).start()
     each(parts, part)
-    each(n_g - 1, lambda g: group_copy(g).wait())
-    each(parts, lambda i: part_copy(i).wait())
+    most = pl.ds(0, (n_g - 1) * SG)
+    pltpu.make_async_copy(w_vmem.at[most], w_hbm.at[most], w_sem).wait()
+    last = pl.ds((n_g - 1) * SG, SG)
+    pltpu.make_async_copy(w_vmem.at[last], w_hbm.at[last], last_sem).wait()
 
 
 def solution(mesh):
@@ -338,7 +336,7 @@
             out_shape=jax.ShapeDtypeStruct(w_vmem.shape, BF16),
             in_specs=[vmem, vmem, vmem],
             out_specs=pl.BlockSpec(memory_space=pl.ANY),
-            scratch_shapes=[pltpu.VMEM((n_ab, SG, n_k // n_ab, n_j, n_i), BF16), dma((n_g,)), dma((n_ab,))],
+            scratch_shapes=[pltpu.VMEM((n_ab, SG, n_k // n_ab, n_j, n_i), BF16), dma, dma],
             compiler_params=pltpu.CompilerParams(vmem_limit_bytes=8 * 1024 * 1024),
         )(w_vmem, a1p, diag_blk)
 

time: 199 us -> 198 us (level)
  no operation moved by 1% of the time
where the time goes in v7:
time: 198 us
  Pallas kernels  198 us (100%)
    pallas_call x1, Pallas kernels, local_step(): pl.pallas_call(kernel, out_shape=(pltpu.VMEM((n_s // 2, n_k, n_j, n_i), B...  192 us
    pallas_call x1, Pallas kernels, local_step(): pl.pallas_call(finish, out_shape=jax.ShapeDtypeStruct(w_vmem.shape, BF16)...  5.82 us

profile of v7, /device:TPU:0, one launch (start us, length us, event | category | flops | bytes accessed | tf_op | source)
XLA Modules:
  0.0 197.7 jit_solution(8894536338188869325)
XLA Ops:
  0.0 0.0 copy-start
  0.0 191.9 %shard_map.55 = (bf16[64,16,64,128]{3,2,1,0:T(8,128)(2,1)S(1)}, bf16[8,128,128]{2,1,0:T(8,128)(2,1)S(1)}) custom-call(bf16[64,64,16,128]{3,2,1,0:T(8,128)(2,1)} %bitcast.1, bf16[128,128]{1,0:T(8,128)(2,1)} %a1_ref.1, bf16[128,128]{1,0:T(8,128)(2,1)} %a2_ref.1, bf16[32,32]{1,0:T(8,128)(2,1)} %a3_ref.1, f32[16,64,128]{2,1,0:T(8,128)} %d_ref.3), custom_call_target="tpu_custom_call" | custom-call | tf_op jit(solution)/shard_map/pallas_call | solution.py:311
  191.9 0.0 copy-done
  191.9 5.8 %shard_map.56 = bf16[64,16,64,128]{3,2,1,0:T(8,128)(2,1)} custom-call(bf16[64,16,64,128]{3,2,1,0:T(8,128)(2,1)S(1)} %get-tuple-element.7.w_vmem, bf16[8,128,128]{2,1,0:T(8,128)(2,1)S(1)} %get-tuple-element.8.a1p_ref, f32[16,64,128]{2,1,0:T(8,128)S(1)} %copy-done), custom_call_target="tpu_custom_call" | custom-call | tf_op jit(solution)/shard_map/pallas_call | solution.py:334
Async XLA Ops:
  0.0 191.9 %copy-start = (f32[16,64,128]{2,1,0:T(8,128)S(1)}, f32[16,64,128]{2,1,0:T(8,128)}, u32[]{:S(2)}) copy-start(f32[16,64,128]{2,1,0:T(8,128)} %d_ref.3) | copy-start | bytes 1572868

commit v8 on v7

--- a/solution.py
+++ b/solution.py
@@ -72,10 +72,10 @@
     lax.fori_loop(0, count * n_jt, body, 0, unroll=count * n_jt)
 
 
-def kernel(x_hbm, a1_ref, a2_ref, a3_ref, d_ref, w_ref, a1p_ref,
+def kernel(x_hbm, a1_hbm, a2_hbm, a3_hbm, d_hbm, w_ref, a1p_ref, d_ref,
            slab, grp, yrecv, u3keep, u3send, xrecv, u2send,
-           l3_ref, a2p_ref,
-           slab_sem, ysend_sem, yrecv_sem, xsend_sem, xrecv_sem, csend_sem, crecv_sem):
+           a1_ref, a2_ref, a3_ref, l3_ref, a2p_ref,
+           fac_sem, slab_sem, ysend_sem, yrecv_sem, xsend_sem, xrecv_sem, csend_sem, crecv_sem):
     m3, m2, m1 = lax.axis_index("m3"), lax.axis_index("m2"), lax.axis_index("m1")
     n_a, n_b, n_l, _ = x_hbm.shape
     n_ab = n_a // AG
@@ -124,6 +124,10 @@
 
     for i in range(FIRST):
         slab_copy(i).start()
+    facs = [pltpu.make_async_copy(src, dst, fac_sem.at[i]) for i, (src, dst) in enumerate(
+        ((a3_hbm, a3_ref), (a2_hbm, a2_ref), (a1_hbm, a1_ref), (d_hbm, d_ref)))]
+    for fac in facs:
+        fac.start()
 
     barrier = pltpu.get_barrier_semaphore()
     for partner in ({"m3": 1 - m3}, {"m2": 1 - m2}, {"m1": 1 - m1}):
@@ -158,6 +162,9 @@
         y_copy(i).start()
 
     each(AHEAD - 1, lambda i: next_piece(i + 1))
+
+    for fac in facs:
+        fac.wait()
 
     k_all, l_all = a3_ref.shape
     rows = k_all * 8
@@ -308,11 +315,12 @@
         n_p = n_b // PB
         vmem = pl.BlockSpec(memory_space=pltpu.VMEM)
         dma = pltpu.SemaphoreType.DMA
-        w_vmem, a1p = pl.pallas_call(
+        w_vmem, a1p, diag = pl.pallas_call(
             kernel,
-            out_shape=(pltpu.VMEM((n_s // 2, n_k, n_j, n_i), BF16), pltpu.VMEM((n_g,) + fac_one.shape, BF16)),
-            in_specs=[pl.BlockSpec(memory_space=pl.ANY), vmem, vmem, vmem, vmem],
-            out_specs=(vmem, vmem),
+            out_shape=(pltpu.VMEM((n_s // 2, n_k, n_j, n_i), BF16), pltpu.VMEM((n_g,) + fac_one.shape, BF16),
+                       pltpu.VMEM(diag_blk.shape, F32)),
+            in_specs=[pl.BlockSpec(memory_space=pl.ANY)] * 5,
+            out_specs=(vmem, vmem, vmem),
             scratch_shapes=[
                 pltpu.VMEM((SLAB_RING, AG, PB, n_l, LANES), BF16),
                 pltpu.VMEM((2 * n_g, n_ab, n_b, n_l, LANES), BF16),
@@ -321,9 +329,12 @@
                 pltpu.VMEM((X_RING, n_p, n_k, PB, LANES), BF16),
                 pltpu.VMEM((n_t, n_p, n_k, PB, LANES), BF16),
                 pltpu.VMEM((C_RING, n_k, n_j, LANES), BF16),
+                pltpu.VMEM(fac_one.shape, BF16),
+                pltpu.VMEM(fac_two.shape, BF16),
+                pltpu.VMEM(fac_three.shape, BF16),
                 pltpu.VMEM((fac_three.shape[0] * 8, 2 * 8 * n_l), BF16),
                 pltpu.VMEM(fac_two.shape, BF16),
-                dma((SLAB_RING,)),
+                dma((4,)), dma((SLAB_RING,)),
                 dma, dma((Y_RING,)),
                 dma((X_RING,)), dma((X_RING,)),
                 dma((C_RING,)), dma((CG_RING,)),
@@ -338,6 +349,6 @@
             out_specs=pl.BlockSpec(memory_space=pl.ANY),
             scratch_shapes=[pltpu.VMEM((n_ab, SG, n_k // n_ab, n_j, n_i), BF16), dma, dma],
             compiler_params=pltpu.CompilerParams(vmem_limit_bytes=8 * 1024 * 1024),
-        )(w_vmem, a1p, diag_blk)
+        )(w_vmem, a1p, diag)
 
     return jax.shard_map(local_step, mesh=mesh, in_specs=(P("dp", "m1", "m2", "m3"), P(), P(), P(), P("m2", "m1", None)), out_specs=P(("dp", "m3"), "m2", "m1", None), check_vma=False)

time: 198 us -> 197 us (level)
  no operation moved by 1% of the time
where the time goes in v8:
time: 197 us
  Pallas kernels  197 us (100%)
    pallas_call x1, Pallas kernels, local_step(): pl.pallas_call(kernel, out_shape=(pltpu.VMEM((n_s // 2, n_k, n_j, n_i), B...  191 us
    pallas_call x1, Pallas kernels, local_step(): pl.pallas_call(finish, out_shape=jax.ShapeDtypeStruct(w_vmem.shape, BF16)...  5.82 us

profile of v8, /device:TPU:0, one launch (start us, length us, event | category | flops | bytes accessed | tf_op | source)
XLA Modules:
  0.0 196.6 jit_solution(7935840029169238577)
XLA Ops:
  0.0 190.8 %shard_map.55 = (bf16[64,16,64,128]{3,2,1,0:T(8,128)(2,1)S(1)}, bf16[8,128,128]{2,1,0:T(8,128)(2,1)S(1)}, f32[16,64,128]{2,1,0:T(8,128)S(1)}) custom-call(bf16[64,64,16,128]{3,2,1,0:T(8,128)(2,1)} %bitcast.1, bf16[128,128]{1,0:T(8,128)(2,1)} %a1_hbm.1, bf16[128,128]{1,0:T(8,128)(2,1)} %a2_hbm.1, bf16[32,32]{1,0:T(8,128)(2,1)} %a3_hbm.1, f32[16,64,128]{2,1,0:T(8,128)} %d_hbm.1), custom_call_target="tpu_custom_call" | custom-call | tf_op jit(solution)/shard_map/pallas_call | solution.py:318
  190.8 5.8 %shard_map.56 = bf16[64,16,64,128]{3,2,1,0:T(8,128)(2,1)} custom-call(bf16[64,16,64,128]{3,2,1,0:T(8,128)(2,1)S(1)} %get-tuple-element.8.w_vmem, bf16[8,128,128]{2,1,0:T(8,128)(2,1)S(1)} %get-tuple-element.9.a1p_ref, f32[16,64,128]{2,1,0:T(8,128)S(1)} %get-tuple-element.10.d_ref), custom_call_target="tpu_custom_call" | custom-call | tf_op jit(solution)/shard_map/pallas_call | solution.py:345

commit v9 on v8

--- a/solution.py
+++ b/solution.py
@@ -14,6 +14,7 @@
 PB = 8
 SLAB_RING = 4
 FIRST = 4
+HEAD = 4
 AHEAD = 7
 Y_RING = 14
 X_RING = 4
@@ -75,7 +76,7 @@
 def kernel(x_hbm, a1_hbm, a2_hbm, a3_hbm, d_hbm, w_ref, a1p_ref, d_ref,
            slab, grp, yrecv, u3keep, u3send, xrecv, u2send,
            a1_ref, a2_ref, a3_ref, l3_ref, a2p_ref,
-           fac_sem, slab_sem, ysend_sem, yrecv_sem, xsend_sem, xrecv_sem, csend_sem, crecv_sem):
+           head_sem, fac_sem, slab_sem, ysend_sem, yrecv_sem, xsend_sem, xrecv_sem, csend_sem, crecv_sem):
     m3, m2, m1 = lax.axis_index("m3"), lax.axis_index("m2"), lax.axis_index("m1")
     n_a, n_b, n_l, _ = x_hbm.shape
     n_ab = n_a // AG
@@ -122,7 +123,17 @@
         here = w_ref.at[pl.ds(g * SG + n_ab, n_ab)]
         return remote("m1", here, here, csend_sem.at[0], crecv_sem.at[g % CG_RING])
 
-    for i in range(FIRST):
+    def head_copy(h):
+        rows = pl.ds(h * HEAD, HEAD)
+        return pltpu.make_async_copy(x_hbm.at[pl.ds(0, AG), rows], slab.at[0, :, rows], head_sem.at[h])
+
+    def head_send(h):
+        rows = pl.ds(h * HEAD, HEAD)
+        return remote("m3", grp.at[(1 - m3) * n_g, 0, rows], yrecv.at[0, 0, rows], ysend_sem, yrecv_sem.at[0])
+
+    for h in range(PB // HEAD):
+        head_copy(h).start()
+    for i in range(1, FIRST):
         slab_copy(i).start()
     facs = [pltpu.make_async_copy(src, dst, fac_sem.at[i]) for i, (src, dst) in enumerate(
         ((a3_hbm, a3_ref), (a2_hbm, a2_ref), (a1_hbm, a1_ref), (d_hbm, d_ref)))]
@@ -133,26 +144,32 @@
     for partner in ({"m3": 1 - m3}, {"m2": 1 - m2}, {"m1": 1 - m1}):
         pl.semaphore_signal(barrier, inc=1, device_id=partner, device_id_type=MESH)
 
-    def regroup(i):
+    def regroup(i, b0=0, count=PB):
         ab, p = i // n_p, i % n_p
         def one_b(b, carry):
+            b = b0 + b
             tiles = skew([slab[i % SLAB_RING, a, b] for a in range(AG)], SG)
             for g in range(2 * n_g):
                 grp[g, ab, p * PB + b] = tiles[g]
             return carry
 
-        lax.fori_loop(0, PB, one_b, 0, unroll=8)
+        lax.fori_loop(0, count, one_b, 0, unroll=count)
+
+        if b0 + count < PB:
+            return
 
         @pl.when(i + SLAB_RING < n_slab)
         def _():
             slab_copy(i + SLAB_RING).start()
 
-    slab_copy(0).wait()
     for i in range(FIRST, SLAB_RING):
         slab_copy(i).start()
-    regroup(0)
-    pl.semaphore_wait(barrier, 3)
-    y_copy(0).start()
+    for h in range(PB // HEAD):
+        head_copy(h).wait()
+        regroup(0, h * HEAD, HEAD)
+        if h == 0:
+            pl.semaphore_wait(barrier, 3)
+        head_send(h).start()
 
     def next_piece(i):
         @pl.when(i < n_slab)
@@ -283,15 +300,15 @@
     parts = wst.shape[0]
     k_part = n_k // parts
 
-    def group_copy(g):
-        here = pl.ds(g * SG, SG)
+    def rhs_copy(i):
+        here = pl.ds(i, 1)
         return pltpu.make_async_copy(w_vmem.at[here], w_hbm.at[here], w_sem)
 
     def part_copy(i):
         return pltpu.make_async_copy(
             wst.at[i], w_hbm.at[pl.ds((n_g - 1) * SG, SG), pl.ds(i * k_part, k_part)], last_sem)
 
-    each(n_g - 1, lambda g: group_copy(g).start())
+    each((n_g - 1) * SG, lambda i: rhs_copy(i).start())
     a1p = a1p_ref[n_g - 1]
 
     def part(i):
@@ -334,7 +351,7 @@
                 pltpu.VMEM(fac_three.shape, BF16),
                 pltpu.VMEM((fac_three.shape[0] * 8, 2 * 8 * n_l), BF16),
                 pltpu.VMEM(fac_two.shape, BF16),
-                dma((4,)), dma((SLAB_RING,)),
+                dma((PB // HEAD,)), dma((4,)), dma((SLAB_RING,)),
                 dma, dma((Y_RING,)),
                 dma((X_RING,)), dma((X_RING,)),
                 dma((C_RING,)), dma((CG_RING,)),

time: 197 us -> 197 us (level)
  no operation moved by 1% of the time
where the time goes in v9:
time: 197 us; the launch traced here: 196 us
  Pallas kernels  196 us (99%)
    pallas_call x1, Pallas kernels, local_step(): pl.pallas_call(kernel, out_shape=(pltpu.VMEM((n_s // 2, n_k, n_j, n_i), B...  191 us
    pallas_call x1, Pallas kernels, local_step(): pl.pallas_call(finish, out_shape=jax.ShapeDtypeStruct(w_vmem.shape, BF16)...  5.8 us

profile of v9, /device:TPU:0, one launch (start us, length us, event | category | flops | bytes accessed | tf_op | source)
XLA Modules:
  0.0 196.5 jit_solution(7684537195308403802)
XLA Ops:
  0.0 190.7 %shard_map.55 = (bf16[64,16,64,128]{3,2,1,0:T(8,128)(2,1)S(1)}, bf16[8,128,128]{2,1,0:T(8,128)(2,1)S(1)}, f32[16,64,128]{2,1,0:T(8,128)S(1)}) custom-call(bf16[64,64,16,128]{3,2,1,0:T(8,128)(2,1)} %bitcast.1, bf16[128,128]{1,0:T(8,128)(2,1)} %a1_hbm.1, bf16[128,128]{1,0:T(8,128)(2,1)} %a2_hbm.1, bf16[32,32]{1,0:T(8,128)(2,1)} %a3_hbm.1, f32[16,64,128]{2,1,0:T(8,128)} %d_hbm.1), custom_call_target="tpu_custom_call" | custom-call | tf_op jit(solution)/shard_map/pallas_call | solution.py:335
  190.7 5.8 %shard_map.56 = bf16[64,16,64,128]{3,2,1,0:T(8,128)(2,1)} custom-call(bf16[64,16,64,128]{3,2,1,0:T(8,128)(2,1)S(1)} %get-tuple-element.8.w_vmem, bf16[8,128,128]{2,1,0:T(8,128)(2,1)S(1)} %get-tuple-element.9.a1p_ref, f32[16,64,128]{2,1,0:T(8,128)S(1)} %get-tuple-element.10.d_ref), custom_call_target="tpu_custom_call" | custom-call | tf_op jit(solution)/shard_map/pallas_call | solution.py:362

commit v10 on v9

--- a/solution.py
+++ b/solution.py
@@ -18,6 +18,7 @@
 AHEAD = 7
 Y_RING = 14
 X_RING = 4
+XS_RING = 2
 C_RING = 2
 CG_RING = 3
 
@@ -107,12 +108,12 @@
         return remote("m3", grp.at[pl.ds((1 - m3) * n_g, n_g)], yrecv, ysend_sem, yrecv_sem.at[0])
 
     def x_copy(t, p):
-        return remote("m2", u3send.at[t % X_RING, p], xrecv.at[t, p],
-                      xsend_sem.at[t % X_RING], xrecv_sem.at[t % X_RING])
+        return remote("m2", u3send.at[t % XS_RING, p], xrecv.at[t, p],
+                      xsend_sem.at[t % XS_RING], xrecv_sem.at[t % X_RING])
 
     def x_all(t):
-        return remote("m2", u3send.at[t % X_RING], xrecv.at[t],
-                      xsend_sem.at[t % X_RING], xrecv_sem.at[t % X_RING])
+        return remote("m2", u3send.at[t % XS_RING], xrecv.at[t],
+                      xsend_sem.at[t % XS_RING], xrecv_sem.at[t % X_RING])
 
     def c_copy(t):
         g = t // n_ab
@@ -169,7 +170,15 @@
         regroup(0, h * HEAD, HEAD)
         if h == 0:
             pl.semaphore_wait(barrier, 3)
-        head_send(h).start()
+        if h == 0:
+            @pl.when(m1 != 0)
+            def _():
+                head_send(0).start()
+        else:
+            @pl.when(m1 == 0)
+            def _():
+                head_send(0).start()
+            head_send(1).start()
 
     def next_piece(i):
         @pl.when(i < n_slab)
@@ -216,7 +225,7 @@
         got = yrecv[g, ab, rows].reshape(PB * n_l, LANES)
         out = dot(l3_ref[...], jnp.concatenate([own, got], axis=0))
         out = out.reshape(2 * n_k, PB, LANES).astype(BF16)
-        u3send[t % X_RING, p] = out[n_k:]
+        u3send[t % XS_RING, p] = out[n_k:]
         u3keep[t % 2, p] = out[:n_k]
 
     def mode_two(t):
@@ -239,9 +248,9 @@
         mode_one_part(here, here, a1p_ref[g], d_ref, part * k_part, part * k_part, k_part)
 
     def step(t, carry):
-        @pl.when((t >= X_RING) & (t < n_t))
-        def _():
-            x_all(t - X_RING).wait_send()
+        @pl.when((t >= XS_RING) & (t < n_t))
+        def _():
+            x_all(t - XS_RING).wait_send()
 
         def piece(p):
             q = t * n_p + p
@@ -289,7 +298,7 @@
     lax.fori_loop(0, n_t + 1, step, 0)
 
     y_all().wait_send()
-    each(X_RING, lambda i: x_all(n_t - X_RING + i).wait_send())
+    each(XS_RING, lambda i: x_all(n_t - XS_RING + i).wait_send())
     each(C_RING, lambda i: c_copy(n_t - C_RING + i).wait_send())
     c_group(n_g - 1).wait_recv()
 
@@ -353,7 +362,7 @@
                 pltpu.VMEM(fac_two.shape, BF16),
                 dma((PB // HEAD,)), dma((4,)), dma((SLAB_RING,)),
                 dma, dma((Y_RING,)),
-                dma((X_RING,)), dma((X_RING,)),
+                dma((XS_RING,)), dma((X_RING,)),
                 dma((C_RING,)), dma((CG_RING,)),
             ],
             compiler_params=pltpu.CompilerParams(

time: 197 us -> 197 us (level)
  no operation moved by 1% of the time
where the time goes in v10:
time: 197 us; the launch traced here: 196 us
  Pallas kernels  196 us (99%)
    pallas_call x1, Pallas kernels, local_step(): pl.pallas_call(kernel, out_shape=(pltpu.VMEM((n_s // 2, n_k, n_j, n_i), B...  191 us
    pallas_call x1, Pallas kernels, local_step(): pl.pallas_call(finish, out_shape=jax.ShapeDtypeStruct(w_vmem.shape, BF16)...  5.8 us

profile of v10, /device:TPU:0, one launch (start us, length us, event | category | flops | bytes accessed | tf_op | source)
XLA Modules:
  0.0 196.4 jit_solution(2622733525157076709)
XLA Ops:
  0.0 190.6 %shard_map.55 = (bf16[64,16,64,128]{3,2,1,0:T(8,128)(2,1)S(1)}, bf16[8,128,128]{2,1,0:T(8,128)(2,1)S(1)}, f32[16,64,128]{2,1,0:T(8,128)S(1)}) custom-call(bf16[64,64,16,128]{3,2,1,0:T(8,128)(2,1)} %bitcast.1, bf16[128,128]{1,0:T(8,128)(2,1)} %a1_hbm.1, bf16[128,128]{1,0:T(8,128)(2,1)} %a2_hbm.1, bf16[32,32]{1,0:T(8,128)(2,1)} %a3_hbm.1, f32[16,64,128]{2,1,0:T(8,128)} %d_hbm.1), custom_call_target="tpu_custom_call" | custom-call | tf_op jit(solution)/shard_map/pallas_call | solution.py:344
  190.6 5.8 %shard_map.56 = bf16[64,16,64,128]{3,2,1,0:T(8,128)(2,1)} custom-call(bf16[64,16,64,128]{3,2,1,0:T(8,128)(2,1)S(1)} %get-tuple-element.8.w_vmem, bf16[8,128,128]{2,1,0:T(8,128)(2,1)S(1)} %get-tuple-element.9.a1p_ref, f32[16,64,128]{2,1,0:T(8,128)S(1)} %get-tuple-element.10.d_ref), custom_call_target="tpu_custom_call" | custom-call | tf_op jit(solution)/shard_map/pallas_call | solution.py:371

commit v11 on v10

--- a/solution.py
+++ b/solution.py
@@ -15,8 +15,8 @@
 SLAB_RING = 4
 FIRST = 4
 HEAD = 4
-AHEAD = 7
-Y_RING = 14
+AHEAD = 6
+Y_RING = 12
 X_RING = 4
 XS_RING = 2
 C_RING = 2

time: 197 us -> 196 us (level)
  no operation moved by 1% of the time
where the time goes in v11:
time: 196 us
  Pallas kernels  196 us (100%)
    pallas_call x1, Pallas kernels, local_step(): pl.pallas_call(kernel, out_shape=(pltpu.VMEM((n_s // 2, n_k, n_j, n_i), B...  191 us
    pallas_call x1, Pallas kernels, local_step(): pl.pallas_call(finish, out_shape=jax.ShapeDtypeStruct(w_vmem.shape, BF16)...  5.8 us

profile of v11, /device:TPU:0, one launch (start us, length us, event | category | flops | bytes accessed | tf_op | source)
XLA Modules:
  0.0 196.4 jit_solution(9455176818878266187)
XLA Ops:
  0.0 190.6 %shard_map.55 = (bf16[64,16,64,128]{3,2,1,0:T(8,128)(2,1)S(1)}, bf16[8,128,128]{2,1,0:T(8,128)(2,1)S(1)}, f32[16,64,128]{2,1,0:T(8,128)S(1)}) custom-call(bf16[64,64,16,128]{3,2,1,0:T(8,128)(2,1)} %bitcast.1, bf16[128,128]{1,0:T(8,128)(2,1)} %a1_hbm.1, bf16[128,128]{1,0:T(8,128)(2,1)} %a2_hbm.1, bf16[32,32]{1,0:T(8,128)(2,1)} %a3_hbm.1, f32[16,64,128]{2,1,0:T(8,128)} %d_hbm.1), custom_call_target="tpu_custom_call" | custom-call | tf_op jit(solution)/shard_map/pallas_call | solution.py:344
  190.6 5.8 %shard_map.56 = bf16[64,16,64,128]{3,2,1,0:T(8,128)(2,1)} custom-call(bf16[64,16,64,128]{3,2,1,0:T(8,128)(2,1)S(1)} %get-tuple-element.8.w_vmem, bf16[8,128,128]{2,1,0:T(8,128)(2,1)S(1)} %get-tuple-element.9.a1p_ref, f32[16,64,128]{2,1,0:T(8,128)S(1)} %get-tuple-element.10.d_ref), custom_call_target="tpu_custom_call" | custom-call | tf_op jit(solution)/shard_map/pallas_call | solution.py:371
